TPU v7x, 32 devices: a whole 2x2x4 slice. The times are simulated.
32 devices in a mesh: expert: 4 (over z), shard: 8 (over y, x, core).
Axes of the slice: x: 2, y: 2, z: 4, core: 2. Of those that a mesh axis runs over, the one named last changes fastest.
Arguments:
- tokens: bfloat16 [768, 4096], P(('expert', 'shard')), may hold values from -0.19921875 to 0.19921875
- expert_ids: int32 [768, 2], P(('expert', 'shard')), may hold values from 0 to 3, all different within a row; in each aligned block of 24 rows (0 to 23, 24 to 47, ...) at most 16 rows name the same one
- weight_gate: bfloat16 [4, 4096, 8192], P('expert', None, 'shard'), may hold values from -0.09375 to 0.09375
- weight_up: bfloat16 [4, 4096, 8192], P('expert', None, 'shard'), may hold values from -0.09375 to 0.09375
- gate_pre: bfloat16 [4, 512, 8192], P('expert', None, 'shard'), may hold values from -8 to 8
- up_pre: bfloat16 [4, 512, 8192], P('expert', None, 'shard'), may hold values from -6 to 6
- hidden_grad: bfloat16 [4, 512, 8192], P('expert', None, 'shard'), may hold values from -6 to 6
Outputs:
- token_grad: bfloat16 [768, 4096], P(('expert', 'shard'))
- gate_weight_grad: float32 [4, 4096, 8192], P('expert', None, 'shard')
- up_weight_grad: float32 [4, 4096, 8192], P('expert', None, 'shard')
Inputs may be any that keep to these rules, and one draw needn't show every extreme that they name: `expert_ids`: each token names 2 different experts. Among the tokens of one device no expert is named more than 16 times, and in every draw some device names some expert exactly 16 times.
All inputs are finite; a program needn't handle non-finite values.
Results may differ from a plain program's by a relative error of at most 0.02.
Values may be sent and summed in bfloat16 or wider, within the bound.
No kernel may reach another device: no remote copies, remote signals or barrier semaphores. Data moves between devices by JAX's collectives and lax.ppermute only.
A program may use at most 192 MiB of HBM per device.

v0:
```python
import jax
import jax.numpy as jnp
from jax import lax
from jax.sharding import PartitionSpec as P


def swiglu_grads(gate_values, up_values, hidden_cotangent):
    gate_float = gate_values.astype(jnp.float32)
    up_float = up_values.astype(jnp.float32)
    cotangent = hidden_cotangent.astype(jnp.float32)
    sigmoid_gate = jax.nn.sigmoid(gate_float)
    gate_grad = (
        cotangent * up_float * sigmoid_gate * (1.0 + gate_float * (1.0 - sigmoid_gate))
    ).astype(jnp.bfloat16)
    up_grad = (cotangent * gate_float * sigmoid_gate).astype(jnp.bfloat16)
    return (gate_grad, up_grad)


def slot_table(expert_ids, groups, capacity):
    token_count = expert_ids.shape[0]
    choices_per = expert_ids.shape[1]
    labels = lax.broadcasted_iota(jnp.int32, (1, 1, groups), 2)
    one_hot = (expert_ids[:, :, None] == labels).astype(jnp.int32)
    flat_hits = one_hot.reshape(token_count * choices_per, groups)
    earlier = jnp.cumsum(flat_hits, axis=0) - flat_hits
    slot_index = jnp.sum(flat_hits * earlier, axis=1).reshape(token_count, choices_per)
    slot_labels = lax.broadcasted_iota(jnp.int32, (1, 1, 1, capacity), 3)
    slot_hits = one_hot[:, :, :, None] * (slot_index[:, :, None, None] == slot_labels).astype(
        jnp.int32
    )
    selection = jnp.sum(slot_hits, axis=1).reshape(token_count, groups * capacity)
    return selection.astype(jnp.bfloat16)


def rows_inner(left_rows, right_rows):
    return lax.dot_general(
        left_rows, right_rows, (((0,), (0,)), ((), ())), preferred_element_type=jnp.float32
    )


def times_transposed(left_rows, weights):
    return lax.dot_general(
        left_rows, weights, (((1,), (1,)), ((), ())), preferred_element_type=jnp.float32
    )


def on_device(tokens, expert_ids, weight_gate, weight_up, gate_pre, up_pre, hidden_grad):
    groups = lax.axis_size("expert")
    shards = lax.axis_size("shard")
    model_width = tokens.shape[1]
    capacity = gate_pre.shape[1] // (groups * shards)
    selection = slot_table(expert_ids, groups, capacity)
    outgoing = rows_inner(selection, tokens).astype(jnp.bfloat16)
    gate_grad, up_grad = swiglu_grads(gate_pre[0], up_pre[0], hidden_grad[0])
    gate_matrix = weight_gate[0]
    up_matrix = weight_up[0]
    arrived = lax.all_to_all(
        outgoing.reshape(groups, capacity, model_width),
        "expert",
        split_axis=0,
        concat_axis=0,
        tiled=True,
    )
    block_rows = lax.all_gather(
        arrived.reshape(groups * capacity, model_width), "shard", axis=0, tiled=True
    )
    gate_rows = gate_grad
    up_rows = up_grad
    gate_wgrad = rows_inner(block_rows, gate_rows)
    up_wgrad = rows_inner(block_rows, up_rows)
    gate_rows = gate_grad
    up_rows = up_grad
    summed = lax.psum_scatter(
        (times_transposed(gate_rows, gate_matrix) + times_transposed(up_rows, up_matrix)).astype(
            jnp.bfloat16
        ),
        "shard",
        scatter_dimension=0,
        tiled=True,
    )
    outbound = summed.reshape(groups, capacity, model_width)
    returned = lax.all_to_all(outbound, "expert", split_axis=0, concat_axis=0, tiled=True)
    returned = returned.reshape(groups * capacity, model_width)
    token_grad = times_transposed(selection, returned.T).astype(jnp.bfloat16)
    return (token_grad, gate_wgrad[None], up_wgrad[None])


def solution(mesh):
    placed = (
        P(("expert", "shard"), None),
        P(("expert", "shard"), None),
        P("expert", None, "shard"),
        P("expert", None, "shard"),
        P("expert", None, "shard"),
        P("expert", None, "shard"),
        P("expert", None, "shard"),
    )
    return jax.shard_map(
        on_device,
        mesh=mesh,
        in_specs=placed,
        out_specs=(
            P(("expert", "shard"), None),
            P("expert", None, "shard"),
            P("expert", None, "shard"),
        ),
        check_vma=False,
    )
```

profile of v0, /device:TPU:0, one launch (start us, length us, event | category | flops | bytes accessed | tf_op | source)
XLA Modules:
  0.0 149.9 jit_solution(7265675212288207498)
XLA Ops:
  7.2 0.0 copy-start
  7.2 0.0 copy-start.5
  7.2 0.0 copy-start.4
  7.2 0.0 copy-start.6
  7.2 0.0 reduce-scatter.2.cloned.1.call-start
  7.3 12.2 %fusion = f32[512,4096]{1,0:T(8,128)} fusion(bf16[1,4096,1024]{2,1,0:T(8,128)(2,1)} %param.10, bf16[1,512,1024]{2,1,0:T(8,128)(2,1)} %param.11, bf16[1,512,1024]{2,1,0:T(8,128)(2,1)} %param.13), kind=kOutput, calls=%fused_computation.2 | convolution fusion | flops 4299161600 | bytes 18874368 | tf_op jit(solution)/shard_map/dot_general | solution.py:42
  19.5 0.0 copy-done.5
  19.5 0.0 copy-done.4
  19.5 0.0 copy-done.6
  19.5 11.3 %add_convert_fusion = bf16[512,4096]{1,0:T(8,128)(2,1)} fusion(f32[512,4096]{1,0:T(8,128)} %fusion, bf16[1,4096,1024]{2,1,0:T(8,128)(2,1)} %param.9, bf16[1,512,1024]{2,1,0:T(8,128)(2,1)S(1)} %copy-done.6, bf16[1,512,1024]{2,1,0:T(8,128)(2,1)S(1)} %copy-done.5, bf16[1,512,1024]{2,1,0:T(8,128)(2,1)S(1)} %copy-done.4), kind=kOutput, calls=%fused_computation.6 | convolution fusion | flops 4305977344 | bytes 24117248 | tf_op jit(solution)/shard_map/dot_general | solution.py:42
  30.8 0.0 copy-start.2
  30.8 0.0 reduce-scatter.2.cloned.1.call-update
  30.8 0.0 all-gather.2.cloned.1.call-start
  30.8 0.6 copy-done.2
  31.4 0.1 copy.14
  31.5 0.1 eq.49
  31.6 0.1 fusion.37
  31.7 0.1 reduce_window_sum.11
  31.8 0.2 select_reduce_fusion
  32.0 0.1 eq.53
  32.1 0.1 copy.15
  32.2 0.0 copy-done
  32.2 0.3 convolution_convert_fusion
  32.5 20.7 %all_to_all.10 = bf16[4,16,4096]{2,1,0:T(8,128)(2,1)} all-to-all(bf16[4,16,4096]{2,1,0:T(8,128)(2,1)S(1)} %bitcast.90), channel_id=1, replica_groups=mesh['expert'=4,'shard'=8] {'expert'}, dimensions={0} | all-to-all | bytes 1048576 | tf_op jit(solution)/shard_map/all_to_all | solution.py:57
  53.2 0.0 all-gather.2.cloned.1.call-update
  53.3 31.6 %reduce-scatter.2.cloned.1.call-done = bf16[64,4096]{1,0:T(8,128)(2,1)} async-done(((bf16[512,4096]{1,0:T(8,128)(2,1)}), bf16[64,4096]{1,0:T(8,128)(2,1)}) %reduce-scatter.2.cloned.1.call-update) | async-done | bytes 524304 | tf_op jit(solution)/shard_map/reduce_scatter | solution.py:73
  84.8 18.9 %all_to_all.11 = bf16[4,16,4096]{2,1,0:T(8,128)(2,1)S(1)} all-to-all(bf16[4,16,4096]{2,1,0:T(8,128)(2,1)} %bitcast.91), channel_id=1, replica_groups=mesh['expert'=4,'shard'=8] {'expert'}, dimensions={0} | all-to-all | bytes 1048576 | tf_op jit(solution)/shard_map/all_to_all | solution.py:82
  103.7 0.9 fusion.6
  104.6 18.7 %all-gather.2.cloned.1.call-done = bf16[512,4096]{1,0:T(8,128)(2,1)} async-done(((bf16[64,4096]{1,0:T(8,128)(2,1)}), bf16[512,4096]{1,0:T(8,128)(2,1)}) %all-gather.2.cloned.1.call-update) | async-done | bytes 4194320 | tf_op jit(solution)/shard_map/all_gather | solution.py:64
  123.3 0.0 copy-start.3
  123.3 11.0 %convolution_bitcast_fusion = f32[1,4096,1024]{2,1,0:T(8,128)} fusion(bf16[512,4096]{1,0:T(8,128)(2,1)} %all-gather.2.cloned.1.call-done, bf16[1,512,1024]{2,1,0:T(8,128)(2,1)S(1)} %copy-done.4, bf16[1,512,1024]{2,1,0:T(8,128)(2,1)S(1)} %copy-done.5), kind=kOutput, calls=%fused_computation | convolution fusion | flops 4299161600 | bytes 23068672 | tf_op jit(solution)/shard_map/dot_general | solution.py:36
  134.3 0.0 copy-done.3
  134.3 0.0 copy-start.1
  134.3 8.8 %convolution_bitcast_fusion.1 = f32[1,4096,1024]{2,1,0:T(8,128)} fusion(bf16[512,4096]{1,0:T(8,128)(2,1)S(1)} %copy-done.3, bf16[1,512,1024]{2,1,0:T(8,128)(2,1)S(1)} %copy-done.6, bf16[1,512,1024]{2,1,0:T(8,128)(2,1)S(1)} %copy-done.5, bf16[1,512,1024]{2,1,0:T(8,128)(2,1)S(1)} %copy-done.4), kind=kOutput, calls=%fused_computation.1 | convolution fusion | flops 4301783040 | bytes 24117248 | tf_op jit(solution)/shard_map/dot_general | solution.py:36
  143.1 0.0 copy-done.1
  (4 shorter events, 0.0 us)
Async XLA Ops:
  7.2 25.0 %copy-start = (bf16[24,4096]{1,0:T(8,128)(2,1)S(1)}, bf16[24,4096]{1,0:T(8,128)(2,1)}, u32[]{:S(2)}) copy-start(bf16[24,4096]{1,0:T(8,128)(2,1)} %param.7) | copy-start | bytes 589828
  7.2 12.3 %copy-start.5 = (bf16[1,512,1024]{2,1,0:T(8,128)(2,1)S(1)}, bf16[1,512,1024]{2,1,0:T(8,128)(2,1)}, u32[]{:S(2)}) copy-start(bf16[1,512,1024]{2,1,0:T(8,128)(2,1)} %param.13) | copy-start | bytes 3145732
  7.2 12.3 %copy-start.4 = (bf16[1,512,1024]{2,1,0:T(8,128)(2,1)S(1)}, bf16[1,512,1024]{2,1,0:T(8,128)(2,1)}, u32[]{:S(2)}) copy-start(bf16[1,512,1024]{2,1,0:T(8,128)(2,1)} %param.11) | copy-start | bytes 3145732
  7.2 12.3 %copy-start.6 = (bf16[1,512,1024]{2,1,0:T(8,128)(2,1)S(1)}, bf16[1,512,1024]{2,1,0:T(8,128)(2,1)}, u32[]{:S(2)}) copy-start(bf16[1,512,1024]{2,1,0:T(8,128)(2,1)} %param.12) | copy-start | bytes 3145732
  7.2 77.6 %reduce-scatter.2.cloned.1.call-start = ((), (), s32[]{:S(2)}) async-start(), calls=%async_computation.3 | async-start | bytes 4718592 | tf_op jit(solution)/shard_map/reduce_scatter | solution.py:73
  30.8 0.7 copy-start.2
  30.8 92.5 %all-gather.2.cloned.1.call-start = ((), (), s32[]{:S(2)}) async-start(), calls=%async_computation.4 | async-start | bytes 4718592 | tf_op jit(solution)/shard_map/all_gather | solution.py:64
  123.3 11.0 %copy-start.3 = (bf16[512,4096]{1,0:T(8,128)(2,1)S(1)}, bf16[512,4096]{1,0:T(8,128)(2,1)}, u32[]{:S(2)}) copy-start(bf16[512,4096]{1,0:T(8,128)(2,1)} %all-gather.2.cloned.1.call-done) | copy-start | bytes 12582916
  134.3 8.8 %copy-start.1 = (bf16[24,4096]{1,0:T(8,128)(2,1)S(1)}, bf16[24,4096]{1,0:T(8,128)(2,1)}, u32[]{:S(2)}) copy-start(bf16[24,4096]{1,0:T(8,128)(2,1)} %param.7) | copy-start | bytes 589828
Sparse Core Ops, SparseCore 0:
  30.9 53.8 reduce-scatter.1
  86.7 36.5 all-gather.1
where the time goes:
time: 150 us
  waiting for transfers between devices  50.2 us (33%)
  matrix products  44.5 us (30%)
  blocking collectives  39.6 us (26%)
  between operations  14.1 us (9%)
    reduce_scatter x1, waiting for transfers between devices, on_device(): lax.psum_scatter((times_transposed(gate_rows, gate_matrix) + times_transp...  31.6 us
    dot_general x3, matrix products, times_transposed(): lax.dot_general(left_rows, weights, (((1,), (1,)), ((), ())), preferred_e...  24.4 us
    all_to_all x1, blocking collectives, on_device(): lax.all_to_all(outgoing.reshape(groups, capacity, model_width), 'expert',...  20.7 us
    dot_general x3, matrix products, rows_inner(): lax.dot_general(left_rows, right_rows, (((0,), (0,)), ((), ())), preferre...  20.1 us
    all_to_all x1, blocking collectives, on_device(): lax.all_to_all(outbound, 'expert', split_axis=0, concat_axis=0, tiled=True)  18.9 us
    all_gather x1, waiting for transfers between devices, on_device(): lax.all_gather(arrived.reshape(groups * capacity, model_width), 'shard',...  18.7 us
  transfers between devices with their start and end apart: 2, of which 2 were waited for; matrix products, arithmetic and copies ran while one was open for 1% of the time, Pallas kernels for 0%

commit v1 on v0

v1 whole, which is shorter than its diff:
```python
import jax
import jax.numpy as jnp
from jax import lax
from jax.experimental import pallas as pl
from jax.experimental.pallas import tpu as pltpu
from jax.sharding import PartitionSpec as P


CHUNKS = 2
FUSED = (False, True)
PARTS = 2
DIRECT = (False, True)


def block_width(width, limit):
    block = min(width, limit)
    while width % block:
        block //= 2
    return block


def times_transposed(left, right):
    return lax.dot_general(left, right, (((1,), (1,)), ((), ())), preferred_element_type=jnp.float32)


def rows_inner(left, right):
    return lax.dot_general(left, right, (((0,), (0,)), ((), ())), preferred_element_type=jnp.float32)


def reverse_bits(value, count):
    return sum(((value >> b) & 1) << (count - 1 - b) for b in range(count))


def core_of(place, shards):
    return lax.rem(place[0], shards) & 1


def swiglu_rows(place, shards, gate_ref, up_ref, hidden_ref, gate_out, up_out, plane, groups, capacity):
    count = len(plane)
    expert = lax.div(place[0], shards)
    shard = lax.rem(place[0], shards)
    core = shard & 1
    for v in range(1 << count):
        masks = [
            sum(bits[b] for b in range(count) if (v >> b) & 1) for bits in (plane, plane[::-1])
        ]
        chip = (shard ^ jnp.where(core == 0, masks[0], masks[1])) - core

        def body(n, carry, v=v, chip=chip):
            source = ((chip + lax.rem(n, 2)) * groups + lax.rem(expert + lax.div(n, 2), groups)) * capacity
            target = (v * groups * 2 + n) * capacity
            rows = pl.ds(pl.multiple_of(source, capacity), capacity)
            to = pl.ds(pl.multiple_of(target, capacity), capacity)
            a = gate_ref[rows, :].astype(jnp.float32)
            b = up_ref[rows, :].astype(jnp.float32)
            g = hidden_ref[rows, :].astype(jnp.float32)
            sig = 1.0 / (1.0 + jnp.exp(-a))
            gs = g * sig
            gate_out[to, :] = (gs * b * (1.0 + a * (1.0 - sig))).astype(jnp.bfloat16)
            up_out[to, :] = (gs * a).astype(jnp.bfloat16)
            return carry

        lax.fori_loop(0, groups * 2, body, 0)


def dgrad_cost(rows, units, width, extra):
    return pl.CostEstimate(
        flops=4 * rows * units * width, transcendentals=0,
        bytes_accessed=4 * rows * units + 4 * units * width + 2 * rows * width + extra,
    )


def dgrad_other(place, shards, sources, weight_gate, weight_up, chunks, plane, groups, capacity):
    rows, units = sources[0].shape
    color_width = weight_gate.shape[0] // 2
    width = color_width // chunks
    block = block_width(width, 512)
    steps = width // block
    count = len(plane)
    chip_rows = rows >> count

    def kernel(place_ref, gate_ref, up_ref, hidden_ref, wg_ref, wu_ref, gate_rows, up_rows, *out_refs):
        @pl.when(pl.program_id(0) == 0)
        def _():
            swiglu_rows(
                place_ref, shards, gate_ref, up_ref, hidden_ref, gate_rows, up_rows,
                plane, groups, capacity,
            )

        acc = times_transposed(gate_rows[...], wg_ref[...])
        acc = (acc + times_transposed(up_rows[...], wu_ref[...])).astype(jnp.bfloat16)
        for chunk, out_ref in enumerate(out_refs):

            @pl.when(pl.program_id(0) // steps == chunk)
            def _(out_ref=out_ref):
                for v in range(1 << count):
                    u = reverse_bits(v, count)
                    out_ref[v * chip_rows : (v + 1) * chip_rows, :] = acc[
                        u * chip_rows : (u + 1) * chip_rows, :
                    ]

    whole = pl.BlockSpec((rows, units), lambda i, place_ref: (0, 0))
    weight = pl.BlockSpec(
        (block, units), lambda i, place_ref: ((1 - core_of(place_ref, shards)) * chunks * steps + i, 0)
    )

    def out_spec(chunk):
        return pl.BlockSpec(
            (rows, block), lambda i, place_ref: (0, jnp.clip(i - chunk * steps, 0, steps - 1))
        )

    grads = jax.ShapeDtypeStruct((rows, units), jnp.bfloat16)
    return pl.pallas_call(
        kernel,
        name="dgrad_other",
        grid_spec=pltpu.PrefetchScalarGridSpec(
            num_scalar_prefetch=1,
            grid=(chunks * steps,),
            in_specs=[whole] * 3 + [weight, weight],
            out_specs=[whole, whole] + [out_spec(c) for c in range(chunks)],
        ),
        out_shape=[grads, grads] + [jax.ShapeDtypeStruct((rows, width), jnp.bfloat16)] * chunks,
        cost_estimate=dgrad_cost(rows, units, color_width, 6 * rows * units),
    )(place, *sources, weight_gate, weight_up)


def dgrad_own(place, shards, gate_rows, up_rows, weight_gate, weight_up, chunk, chunks, came):
    rows, units = gate_rows.shape
    width = weight_gate.shape[0] // (2 * chunks)
    block = block_width(width, 512)
    steps = width // block
    middle = rows // 2

    def kernel(place_ref, gate_ref, up_ref, wg_ref, wu_ref, *refs):
        high_ref, low_ref = refs[-2:]
        acc = times_transposed(gate_ref[...], wg_ref[...])
        acc = acc + times_transposed(up_ref[...], wu_ref[...])
        if came:
            acc = acc + refs[0][...].astype(jnp.float32)
        low_ref[...] = acc[:middle].astype(jnp.bfloat16)
        high_ref[...] = acc[middle:].astype(jnp.bfloat16)

    whole = pl.BlockSpec((rows, units), lambda i, place_ref: (0, 0))
    weight = pl.BlockSpec(
        (block, units), lambda i, place_ref: ((core_of(place_ref, shards) * chunks + chunk) * steps + i, 0)
    )
    column = lambda i, place_ref: (0, i)
    return pl.pallas_call(
        kernel,
        grid_spec=pltpu.PrefetchScalarGridSpec(
            num_scalar_prefetch=1,
            grid=(steps,),
            in_specs=[whole, whole, weight, weight] + [pl.BlockSpec((rows, block), column)] * len(came),
            out_specs=[pl.BlockSpec((middle, block), column)] * 2,
        ),
        out_shape=[jax.ShapeDtypeStruct((middle, width), jnp.bfloat16)] * 2,
        cost_estimate=dgrad_cost(rows, units, width, 0),
    )(place, gate_rows, up_rows, weight_gate, weight_up, *came)


def wgrad(place, shards, own_pieces, other_pieces, gate_rows, up_rows, part, parts, into):
    rows, units = gate_rows.shape
    pieces = len(own_pieces)
    piece_rows, width = own_pieces[0].shape
    block = block_width(width, 512)
    steps = width // block

    def kernel(place_ref, *refs):
        gate_ref, up_ref = refs[2 * pieces : 2 * pieces + 2]
        gate_out, up_out, left_ref = refs[-3:]

        def gather(piece_refs):
            for n, ref in enumerate(piece_refs):
                left_ref[n * piece_rows : (n + 1) * piece_rows, :] = ref[...]

        @pl.when(pl.program_id(0) < steps)
        def _():
            gather(refs[:pieces])

        @pl.when(pl.program_id(0) >= steps)
        def _():
            gather(refs[pieces : 2 * pieces])

        gate_out[...] = rows_inner(left_ref[...], gate_ref[...])
        up_out[...] = rows_inner(left_ref[...], up_ref[...])

    def out_index(i, place_ref):
        core = core_of(place_ref, shards)
        color = jnp.where(i < steps, core, 1 - core)
        return ((color * parts + part) * steps + lax.rem(i, steps), 0)

    whole = pl.BlockSpec((rows, units), lambda i, place_ref: (0, 0))
    own = pl.BlockSpec((piece_rows, block), lambda i, place_ref: (0, jnp.minimum(i, steps - 1)))
    other = pl.BlockSpec((piece_rows, block), lambda i, place_ref: (0, jnp.maximum(i - steps, 0)))
    out = pl.BlockSpec((block, units), out_index)
    operands = (place, *own_pieces, *other_pieces, gate_rows, up_rows, *into)
    return pl.pallas_call(
        kernel,
        grid_spec=pltpu.PrefetchScalarGridSpec(
            num_scalar_prefetch=1,
            grid=(2 * steps,),
            in_specs=[own] * pieces
            + [other] * pieces
            + [whole, whole]
            + [pl.BlockSpec(memory_space=pl.ANY)] * len(into),
            out_specs=[out, out],
            scratch_shapes=[pltpu.VMEM((rows, block), jnp.bfloat16)],
        ),
        out_shape=[jax.ShapeDtypeStruct((2 * parts * width, units), jnp.float32)] * 2,
        input_output_aliases={len(operands) - len(into) + n: n for n in range(len(into))},
        cost_estimate=pl.CostEstimate(
            flops=8 * rows * units * width, transcendentals=0,
            bytes_accessed=4 * rows * units + 4 * rows * width + 16 * units * width,
        ),
    )(*operands)


def in_hbm(value):
    return pltpu.with_memory_space_constraint(value, pltpu.HBM)


def total(terms):
    value = terms[0].astype(jnp.float32)
    for term in terms[1:]:
        value = value + term.astype(jnp.float32)
    return value.astype(jnp.bfloat16)


def on_device(tokens, expert_ids, weight_gate, weight_up, gate_pre, up_pre, hidden_grad):
    groups = lax.axis_size("expert")
    shards = lax.axis_size("shard")
    expert = lax.axis_index("expert")
    shard = lax.axis_index("shard")
    token_count, model_width = tokens.shape
    capacity = gate_pre.shape[1] // (groups * shards)
    half = model_width // 2
    width = half // CHUNKS
    bits = [1 << b for b in range(shards.bit_length() - 1)]
    assert 1 << len(bits) == shards
    plane = bits[1:]
    count = len(plane)
    core = shard & 1
    place = (expert * shards + shard).astype(jnp.int32).reshape(1)

    def over_core(value):
        return lax.ppermute(value, "shard", [(i, i ^ 1) for i in range(shards)])

    def over_plane(value, v):
        masks = [
            sum(bits[b] for b in range(count) if (v >> b) & 1) for bits in (plane, plane[::-1])
        ]
        return lax.ppermute(value, "shard", [(i, i ^ masks[i & 1]) for i in range(shards)])

    def over_expert(value, step):
        return lax.ppermute(value, "expert", [(i, (i + step) % groups) for i in range(groups)])

    def by_core(first, second):
        return jnp.where(core == 0, first, second)

    peer_tokens = over_core(tokens)
    peer_ids = over_core(expert_ids)
    both = jnp.concatenate([tokens, peer_tokens], axis=0)
    both = by_core(both[:, :half], both[:, half:])
    both_ids = jnp.concatenate([expert_ids, peer_ids], axis=0)

    relative = lax.rem(expert - both_ids + groups, groups)
    shape = (2 * token_count, groups * 2 * capacity)
    column = lax.broadcasted_iota(jnp.int32, shape, 1)
    token = lax.broadcasted_iota(jnp.int32, shape, 0)
    distance = column // (2 * capacity)
    named = jnp.any(relative[:, :, None] == distance[:, None, :], axis=1)
    named = named & (token // token_count ^ core == column // capacity % 2)
    named = named.astype(jnp.bfloat16)
    square = (2 * token_count, 2 * token_count)
    lower = lax.broadcasted_iota(jnp.int32, square, 0) > lax.broadcasted_iota(jnp.int32, square, 1)
    earlier = lax.dot_general(
        lower.astype(jnp.bfloat16), named, (((1,), (0,)), ((), ())), preferred_element_type=jnp.float32
    )
    selection = jnp.where(earlier == (column % capacity).astype(jnp.float32), named, 0)

    outgoing = rows_inner(selection, both).astype(jnp.bfloat16)
    outgoing = outgoing.reshape(groups, 2 * capacity, half)
    arrived = [outgoing[0]]
    for k in range(1, groups):
        arrived.append(over_expert(outgoing[k], groups - k))

    weights = (weight_gate[0], weight_up[0])
    gate_rows, up_rows, *away = dgrad_other(
        place, shards, (gate_pre[0], up_pre[0], hidden_grad[0]), *weights, CHUNKS,
        plane, groups, capacity,
    )
    came = []
    for chunk in range(CHUNKS):
        came.append(over_core(away[chunk]))
    terms, got = [], []
    for chunk in range(CHUNKS):
        added = (in_hbm(came[chunk]),) if FUSED[chunk] else ()
        high, low = dgrad_own(place, shards, gate_rows, up_rows, *weights, chunk, CHUNKS, added)
        high, low = [high], [low]
        if not added:
            middle = came[chunk].shape[0] // 2
            high.append(came[chunk][middle:])
            low.append(came[chunk][:middle])
        got = over_plane(total(high) if len(high) > 1 else high[0], 1 << count - 1)
        terms.append(low + [got])
    for b in range(count - 1)[::-1]:
        middle = terms[0][0].shape[0] // 2
        sums = [total([t[middle:] for t in chunk_terms]) for chunk_terms in terms]
        joined = over_plane(jnp.concatenate(sums, axis=1), 1 << b)
        terms = [
            [t[:middle] for t in chunk_terms] + [joined[:, c * width : (c + 1) * width]]
            for c, chunk_terms in enumerate(terms)
        ]
    summed = jnp.concatenate([total(chunk_terms) for chunk_terms in terms], axis=1)

    masks = range(1 << count)
    grads = ()
    part_width = half // PARTS
    for part in range(PARTS):
        columns = slice(part * part_width, (part + 1) * part_width)
        held = {0: jnp.concatenate([rows[:, columns] for rows in arrived], axis=0)}
        for v in masks[1:]:
            bit = v if DIRECT[part] else 1 << v.bit_length() - 1
            held[v] = over_plane(held[v ^ bit], bit)
        swapped = {}
        for v in masks:
            swapped[v] = over_core(held[v])
        grads = wgrad(
            place,
            shards,
            [in_hbm(held[v]) for v in masks],
            [in_hbm(swapped[reverse_bits(v, count)]) for v in masks],
            in_hbm(gate_rows),
            in_hbm(up_rows),
            part,
            PARTS,
            grads,
        )
    gate_wgrad, up_wgrad = grads

    blocks = summed.reshape(groups, 2 * capacity, half)
    back = [blocks[0]]
    for k in range(1, groups):
        back.append(over_expert(blocks[k], k))
    combined = lax.dot_general(
        selection, jnp.concatenate(back, axis=0), (((1,), (0,)), ((), ())),
        preferred_element_type=jnp.float32,
    ).astype(jnp.bfloat16)
    kept = combined[:token_count]
    got = over_core(combined[token_count:])
    token_grad = jnp.concatenate([by_core(kept, got), by_core(got, kept)], axis=1)
    return (token_grad, gate_wgrad[None], up_wgrad[None])


def solution(mesh):
    placed = (
        P(("expert", "shard"), None),
        P(("expert", "shard"), None),
        P("expert", None, "shard"),
        P("expert", None, "shard"),
        P("expert", None, "shard"),
        P("expert", None, "shard"),
        P("expert", None, "shard"),
    )

    return jax.shard_map(
        on_device,
        mesh=mesh,
        in_specs=placed,
        out_specs=(
            P(("expert", "shard"), None),
            P("expert", None, "shard"),
            P("expert", None, "shard"),
        ),
        check_vma=False,
    )
```

time: 150 us -> 110 us (0.73); the launches traced: 150 us -> 108 us
  matrix products: 44.5 us -> 1.65 us
  Pallas kernels: 0 us -> 41.8 us
  blocking collectives: 39.6 us -> 0 us
  starting transfers between devices: 0.08 us -> 22.2 us
  waiting for transfers between devices: 50.2 us -> 32 us
  between operations: 14.1 us -> 1.07 us
  other arithmetic: 0.37 us -> 5.69 us
  local copies, waits for them, and re-layouts: 0.99 us -> 3.66 us
    dot_general x6 -> x3, matrix products: 44.5 us -> 1.65 us  [the longest x1 1.12 us: on_device(): lax.dot_general(selection, jnp.concatenate(back, axis=0), (((1,), (0,)),...]
    pallas_call x0 -> x5, Pallas kernels: none -> 41.8 us  [the longest x2 18.6 us: wgrad(): pl.pallas_call(kernel, grid_spec=pltpu.PrefetchScalarGridSpec(num_scalar_...]
    all_to_all x2 -> x0, blocking collectives: 39.6 us -> none  [the longest x1 20.7 us: on_device(): lax.all_to_all(outgoing.reshape(groups, capacity, model_width), 'expert',...]
    ppermute x0 -> x28, waiting for transfers between devices: none -> 32 us  [the longest x9 25.8 us: over_plane(): lax.ppermute(value, 'shard', [(i, i ^ masks[i & 1]) for i in range(shards)])]
    reduce_scatter x1 -> x0, waiting for transfers between devices: 31.6 us -> none  [on_device(): lax.psum_scatter((times_transposed(gate_rows, gate_matrix) + times_transp...]
    ppermute x0 -> x28, starting transfers between devices: none -> 22.2 us  [the longest x6 10.5 us: over_expert(): lax.ppermute(value, 'expert', [(i, (i + step) % groups) for i in range(gr...]
    all_gather x1 -> x0, waiting for transfers between devices: 18.7 us -> none  [on_device(): lax.all_gather(arrived.reshape(groups * capacity, model_width), 'shard',...]
    convert_element_type x4, other arithmetic: 0.1 us -> 4.65 us  [total(): return value.astype(jnp.bfloat16)]
  transfers between devices with their start and end apart: 2 -> 28, of which waited for: 2 -> 7; matrix products, arithmetic and copies ran while one was open for 1% -> 8% of each run, Pallas kernels for 0% -> 39%
where the time goes in v1:
time: 110 us; the launch traced here: 108 us
  Pallas kernels  41.8 us (38%)
  waiting for transfers between devices  32 us (29%)
  starting transfers between devices  22.2 us (20%)
  other arithmetic  5.69 us (5%)
  local copies, waits for them, and re-layouts  3.66 us (3%)
  matrix products  1.65 us (2%)
    ppermute x9, waiting for transfers between devices, over_plane(): lax.ppermute(value, 'shard', [(i, i ^ masks[i & 1]) for i in range(shards)])  25.8 us
    pallas_call x2, Pallas kernels, wgrad(): pl.pallas_call(kernel, grid_spec=pltpu.PrefetchScalarGridSpec(num_scalar_...  18.6 us
    pallas_call x1, Pallas kernels, dgrad_other(): pl.pallas_call(kernel, name='dgrad_other', grid_spec=pltpu.PrefetchScalar...  11.7 us
    pallas_call x2, Pallas kernels, dgrad_own(): pl.pallas_call(kernel, grid_spec=pltpu.PrefetchScalarGridSpec(num_scalar_...  11.6 us
    ppermute x6, starting transfers between devices, over_expert(): lax.ppermute(value, 'expert', [(i, (i + step) % groups) for i in range(gr...  10.5 us
    ppermute x9, starting transfers between devices, over_plane(): lax.ppermute(value, 'shard', [(i, i ^ masks[i & 1]) for i in range(shards)])  9.83 us
    ppermute x6, waiting for transfers between devices, over_expert(): lax.ppermute(value, 'expert', [(i, (i + step) % groups) for i in range(gr...  6.2 us
    convert_element_type x4, other arithmetic, total(): return value.astype(jnp.bfloat16)  4.65 us
  transfers between devices with their start and end apart: 28, of which 7 were waited for; matrix products, arithmetic and copies ran while one was open for 8% of the time, Pallas kernels for 39%

profile of v1, /device:TPU:0, one launch (start us, length us, event | category | flops | bytes accessed | tf_op | source)
XLA Modules:
  0.0 108.1 jit_solution(17566991389344590243)
XLA Ops:
  0.6 0.6 collective-permute-start
  1.2 0.1 collective-permute-start.10
  1.3 11.7 %dgrad_other.1 = (bf16[512,1024]{1,0:T(8,128)(2,1)}, bf16[512,1024]{1,0:T(8,128)(2,1)}, bf16[512,1024]{1,0:T(8,128)(2,1)}, bf16[512,1024]{1,0:T(8,128)(2,1)}) custom-call(s32[1]{0:T(128)} %bitcast.place_ref, bf16[512,1024]{1,0:T(8,128)(2,1)} %bitcast.18, bf16[512,1024]{1,0:T(8,128)(2,1)} %bitcast.19, bf16[512,1024]{1,0:T(8,128)(2,1)} %bitcast.20, ...), custom_call_target="tpu_custom_call" | custom-call | flops 4294967296 | bytes 15728640 | tf_op jit(solution)/shard_map/dgrad_other/pallas_call | solution.py:113
  13.0 0.4 collective-permute-start.1
  13.6 5.6 %shard_map.94 = (bf16[256,1024]{1,0:T(8,128)(2,1)}, bf16[256,1024]{1,0:T(8,128)(2,1)}) custom-call(s32[1]{0:T(128)} %bitcast.place_ref, bf16[512,1024]{1,0:T(8,128)(2,1)} %get-tuple-element.15.gate_ref.refs_8_, bf16[512,1024]{1,0:T(8,128)(2,1)} %get-tuple-element.16.up_ref.refs_9_, bf16[4096,1024]{1,0:T(8,128)(2,1)} %bitcast.11, bf16[4096,1024]{1,0:T(8,128)(2,1)} %bitcast.14), custom_call_target="tpu_custom_call" | custom-call | flops 2147483648 | bytes 7340032 | tf_op jit(solution)/shard_map/pallas_call | solution.py:148
  19.2 0.1 compare_select_fusion
  19.3 0.1 compare_reduce_fusion
  19.4 0.2 fusion
  19.6 0.3 convolution_convert_fusion
  20.0 0.8 fusion.34
  20.7 5.0 %collective-permute-start.11 = (bf16[32,2048]{1,0:T(8,128)(2,1)}, bf16[32,2048]{1,0:T(8,128)(2,1)}, u32[]{:S(2)}, u32[]{:S(2)}) collective-permute-start(bf16[32,2048]{1,0:T(8,128)(2,1)} %get-tuple-element.29), channel_id=1, source_target_pairs={{0,24},{8,0},{16,8},{24,16},{1,25},{9,1},{17,9},{25,17},{2,26},{10... | collective-permute-start | bytes 393224 | tf_op jit(solution)/shard_map/ppermute | solution.py:255
  25.7 1.0 collective-permute-start.12
  26.8 1.2 %add_convert_fusion = bf16[256,1024]{1,0:T(8,128)(2,1)S(1)} fusion(bf16[256,1024]{1,0:T(8,128)(2,1)} %get-tuple-element.19, bf16[512,1024]{1,0:T(8,128)(2,1)S(1)} %collective-permute-done.1), kind=kLoop, calls=%fused_computation.4 | loop fusion | flops 1048576 | bytes 1572864 | tf_op jit(solution)/shard_map/convert_element_type | solution.py:226
  28.0 1.6 %collective-permute-start.2 = (bf16[256,1024]{1,0:T(8,128)(2,1)S(1)}, bf16[256,1024]{1,0:T(8,128)(2,1)}, u32[]{:S(2)}, u32[]{:S(2)}) collective-permute-start(bf16[256,1024]{1,0:T(8,128)(2,1)S(1)} %add_convert_fusion), channel_id=1, source_target_pairs={{0,4},{1,3},{2,6},{3,1},{4,0},{5,7},{6,2},{7,5},{8,12},{9,11},{10,... | collective-permute-start | bytes 1572872 | tf_op jit(solution)/shard_map/ppermute | solution.py:252
  29.6 1.0 copy-done.1
  30.6 6.0 %shard_map.95 = (bf16[256,1024]{1,0:T(8,128)(2,1)}, bf16[256,1024]{1,0:T(8,128)(2,1)}) custom-call(s32[1]{0:T(128)} %bitcast.place_ref, bf16[512,1024]{1,0:T(8,128)(2,1)} %get-tuple-element.15.gate_ref.refs_8_, bf16[512,1024]{1,0:T(8,128)(2,1)} %get-tuple-element.16.up_ref.refs_9_, bf16[4096,1024]{1,0:T(8,128)(2,1)} %bitcast.12, ...), custom_call_target="tpu_custom_call" | custom-call | flops 2147483648 | bytes 7340032 | tf_op jit(solution)/shard_map/pallas_call | solution.py:148
  36.6 0.5 collective-permute-start.4
  37.1 0.9 fusion.35
  38.0 1.1 add_convert_fusion.4
  39.1 6.9 %collective-permute-done.4 = bf16[256,1024]{1,0:T(8,128)(2,1)S(1)} collective-permute-done((bf16[256,1024]{1,0:T(8,128)(2,1)}, bf16[256,1024]{1,0:T(8,128)(2,1)S(1)}, u32[]{:S(2)}, u32[]{:S(2)}) %collective-permute-start.4) | collective-permute-done | bytes 524320 | tf_op jit(solution)/shard_map/ppermute | solution.py:252
  45.9 1.0 add_convert_fusion.3
  47.0 1.6 %collective-permute-start.5 = (bf16[128,2048]{1,0:T(8,128)(2,1)S(1)}, bf16[128,2048]{1,0:T(8,128)(2,1)S(1)}, u32[]{:S(2)}, u32[]{:S(2)}) collective-permute-start(bf16[128,2048]{1,0:T(8,128)(2,1)S(1)} %pad_maximum_fusion), channel_id=1, source_target_pairs={{0,2},{1,5},{2,0},{3,7},{4,6},{5,1},{6,4},{7,3},{8,10},{9,13},{10,... | collective-permute-start | bytes 1572872 | tf_op jit(solution)/shard_map/ppermute | solution.py:252
  48.6 0.5 collective-permute-start.16
  49.2 1.6 %collective-permute-start.21 = (bf16[128,1024]{1,0:T(8,128)(2,1)S(1)}, bf16[128,1024]{1,0:T(8,128)(2,1)S(1)}, u32[]{:S(2)}, u32[]{:S(2)}) collective-permute-start(bf16[128,1024]{1,0:T(8,128)(2,1)S(1)} %pad_maximum_fusion.2.refs_0_), channel_id=1, source_target_pairs={{0,2},{1,5},{2,0},{3,7},{4,6},{5,1},{6,4},{7,3},{8,10},{9,13},{10,... | collective-permute-start | bytes 786440 | tf_op jit(solution)/shard_map/ppermute | solution.py:252
  50.8 1.5 %collective-permute-start.15 = (bf16[128,1024]{1,0:T(8,128)(2,1)S(1)}, bf16[128,1024]{1,0:T(8,128)(2,1)S(1)}, u32[]{:S(2)}, u32[]{:S(2)}) collective-permute-start(bf16[128,1024]{1,0:T(8,128)(2,1)S(1)} %pad_maximum_fusion.1.refs_0_), channel_id=1, source_target_pairs={{0,4},{1,3},{2,6},{3,1},{4,0},{5,7},{6,2},{7,5},{8,12},{9,11},{10,... | collective-permute-start | bytes 786440 | tf_op jit(solution)/shard_map/ppermute | solution.py:252
  52.3 0.5 collective-permute-start.14
  52.8 11.4 %collective-permute-done.16.refs_3_ = bf16[128,1024]{1,0:T(8,128)(2,1)S(1)} collective-permute-done((bf16[128,1024]{1,0:T(8,128)(2,1)S(1)}, bf16[128,1024]{1,0:T(8,128)(2,1)S(1)}, u32[]{:S(2)}, u32[]{:S(2)}) %collective-permute-start.16) | collective-permute-done | bytes 262176 | tf_op jit(solution)/shard_map/ppermute | solution.py:252
  64.2 1.8 %collective-permute-done.21.refs_1_ = bf16[128,1024]{1,0:T(8,128)(2,1)S(1)} collective-permute-done((bf16[128,1024]{1,0:T(8,128)(2,1)S(1)}, bf16[128,1024]{1,0:T(8,128)(2,1)S(1)}, u32[]{:S(2)}, u32[]{:S(2)}) %collective-permute-start.21) | collective-permute-done | bytes 262176 | tf_op jit(solution)/shard_map/ppermute | solution.py:252
  66.0 1.5 %collective-permute-start.22 = (bf16[128,1024]{1,0:T(8,128)(2,1)S(1)}, bf16[128,1024]{1,0:T(8,128)(2,1)S(1)}, u32[]{:S(2)}, u32[]{:S(2)}) collective-permute-start(bf16[128,1024]{1,0:T(8,128)(2,1)S(1)} %pad_maximum_fusion.2.refs_0_), channel_id=1, source_target_pairs={{0,4},{1,3},{2,6},{3,1},{4,0},{5,7},{6,2},{7,5},{8,12},{9,11},{10,... | collective-permute-start | bytes 786440 | tf_op jit(solution)/shard_map/ppermute | solution.py:252
  67.5 0.6 collective-permute-start.23
  68.0 1.3 %add_convert_fusion.2 = (bf16[128,1024]{1,0:T(8,128)(2,1)S(1)}, bf16[128,1024]{1,0:T(8,128)(2,1)S(1)}) fusion(bf16[128,2048]{1,0:T(8,128)(2,1)S(1)} %collective-permute-done.5, bf16[256,1024]{1,0:T(8,128)(2,1)} %collective-permute-done.2, bf16[512,1024]{1,0:T(8,128)(2,1)S(1)} %collective-permute-done.1, bf16[256,1024]{1,0:T(8,128)(2,1)S(1)} %copy-done.2, ...), kind=kLoop, calls=%fused_computation.20 | loop fusion | flops 1835008 | bytes 2359296 | tf_op jit(solution)/shard_map/convert_element_type | solution.py:226
  69.5 2.9 %collective-permute-done.22.refs_2_ = bf16[128,1024]{1,0:T(8,128)(2,1)S(1)} collective-permute-done((bf16[128,1024]{1,0:T(8,128)(2,1)S(1)}, bf16[128,1024]{1,0:T(8,128)(2,1)S(1)}, u32[]{:S(2)}, u32[]{:S(2)}) %collective-permute-start.22) | collective-permute-done | bytes 262176 | tf_op jit(solution)/shard_map/ppermute | solution.py:252
  72.4 2.8 %collective-permute-done.23.refs_3_ = bf16[128,1024]{1,0:T(8,128)(2,1)S(1)} collective-permute-done((bf16[128,1024]{1,0:T(8,128)(2,1)S(1)}, bf16[128,1024]{1,0:T(8,128)(2,1)S(1)}, u32[]{:S(2)}, u32[]{:S(2)}) %collective-permute-start.23) | collective-permute-done | bytes 262176 | tf_op jit(solution)/shard_map/ppermute | solution.py:252
  75.2 3.4 %collective-permute-start.6 = (bf16[32,2048]{1,0:T(8,128)(2,1)S(1)}, bf16[32,2048]{1,0:T(8,128)(2,1)S(1)}, u32[]{:S(2)}, u32[]{:S(2)}) collective-permute-start(bf16[32,2048]{1,0:T(8,128)(2,1)S(1)} %get-tuple-element.33), channel_id=1, source_target_pairs={{0,8},{8,16},{16,24},{24,0},{1,9},{9,17},{17,25},{25,1},{2,10},{10... | collective-permute-start | bytes 393224 | tf_op jit(solution)/shard_map/ppermute | solution.py:255
  78.7 0.5 collective-permute-start.8
  79.2 0.5 collective-permute-start.20
  79.7 0.1 collective-permute-start.18
  79.7 3.7 %collective-permute-done.6 = bf16[32,2048]{1,0:T(8,128)(2,1)S(1)} collective-permute-done((bf16[32,2048]{1,0:T(8,128)(2,1)S(1)}, bf16[32,2048]{1,0:T(8,128)(2,1)S(1)}, u32[]{:S(2)}, u32[]{:S(2)}) %collective-permute-start.6) | collective-permute-done | bytes 131104 | tf_op jit(solution)/shard_map/ppermute | solution.py:255
  83.5 2.5 %collective-permute-done.8 = bf16[32,2048]{1,0:T(8,128)(2,1)} collective-permute-done((bf16[32,2048]{1,0:T(8,128)(2,1)S(1)}, bf16[32,2048]{1,0:T(8,128)(2,1)}, u32[]{:S(2)}, u32[]{:S(2)}) %collective-permute-start.8) | collective-permute-done | bytes 131104 | tf_op jit(solution)/shard_map/ppermute | solution.py:255
  85.9 0.6 collective-permute-start.7
  86.6 9.3 %shard_map.96 = (f32[4096,1024]{1,0:T(8,128)}, f32[4096,1024]{1,0:T(8,128)}) custom-call(s32[1]{0:T(128)} %bitcast.place_ref, bf16[128,1024]{1,0:T(8,128)(2,1)} %copy-done.9, bf16[128,1024]{1,0:T(8,128)(2,1)} %copy-done.12, bf16[128,1024]{1,0:T(8,128)(2,1)} %copy-done.14, bf16[128,1024]{1,0:T(8,128)(2,1)} %copy-done.15, bf16[128,1024]{1,0:T(8,128)(2,1)} %copy-done.13, ...), custom_call_target="tpu_custom_call" | custom-call | flops 4294967296 | bytes 20971520 | tf_op jit(solution)/shard_map/pallas_call | solution.py:197
  95.9 1.1 %convolution_convert_fusion.1 = bf16[48,2048]{1,0:T(8,128)(2,1)S(1)} fusion(bf16[48,128]{1,0:T(8,128)(2,1)S(1)} %fusion, bf16[32,2048]{1,0:T(8,128)(2,1)} %collective-permute-done.8, bf16[32,2048]{1,0:T(8,128)(2,1)S(1)} %collective-permute-done.7, bf16[32,2048]{1,0:T(8,128)(2,1)S(1)} %collective-permute-done.6, bf16[32,2048]{1,0:T(8,128)(2,1)S(1)} %get-tuple-element.32), kind=kOutput, calls=%fused_computation.1 | convolution fusion | flops 27361280 | bytes 733184 | tf_op jit(solution)/shard_map/dot_general | solution.py:345
  97.2 0.6 copy-done.5
  97.8 0.1 copy-done.6
  97.9 0.1 copy-done.7
  98.0 0.1 copy-done.8
  98.1 9.3 %shard_map.97 = (f32[4096,1024]{1,0:T(8,128)}, f32[4096,1024]{1,0:T(8,128)}) custom-call(s32[1]{0:T(128)} %bitcast.place_ref, bf16[128,1024]{1,0:T(8,128)(2,1)} %copy-done, bf16[128,1024]{1,0:T(8,128)(2,1)} %collective-permute-done.14.refs_1_, bf16[128,1024]{1,0:T(8,128)(2,1)} %copy-done.4, ...), custom_call_target="tpu_custom_call", output_to_operand_aliasing={{0}: (11, {}), {1}: (12, {})} | custom-call | flops 4294967296 | bytes 20971520 | tf_op jit(solution)/shard_map/pallas_call | solution.py:197
  107.4 0.7 pad_maximum_fusion.3
  (82 shorter events, 0.6 us)
Async XLA Ops:
  0.6 12.9 %copy-start.10 = (bf16[24,4096]{1,0:T(8,128)(2,1)S(1)}, bf16[24,4096]{1,0:T(8,128)(2,1)}, u32[]{:S(2)}) copy-start(bf16[24,4096]{1,0:T(8,128)(2,1)} %param.7) | copy-start | bytes 589828
  0.6 18.6 %collective-permute-start = (s32[24,2]{0,1:T(2,128)}, s32[24,2]{0,1:T(2,128)S(1)}, u32[]{:S(2)}, u32[]{:S(2)}) collective-permute-start(s32[24,2]{0,1:T(2,128)} %param.8), channel_id=1, source_target_pairs={{0,1},{1,0},{2,3},{3,2},{4,5},{5,4},{6,7},{7,6},{8,9},{9,8},{10,11... | collective-permute-start | bytes 584 | tf_op jit(solution)/shard_map/ppermute | solution.py:246
  1.2 18.4 %collective-permute-start.10 = (bf16[24,4096]{1,0:T(8,128)(2,1)}, bf16[24,4096]{1,0:T(8,128)(2,1)S(1)}, u32[]{:S(2)}, u32[]{:S(2)}) collective-permute-start(bf16[24,4096]{1,0:T(8,128)(2,1)} %param.7), channel_id=1, source_target_pairs={{0,1},{1,0},{2,3},{3,2},{4,5},{5,4},{6,7},{7,6},{8,9},{9,8},{10,11... | collective-permute-start | bytes 589832 | tf_op jit(solution)/shard_map/ppermute | solution.py:246
  1.3 17.9 %copy-start.11 = (s32[24,2]{0,1:T(2,128)S(1)}, s32[24,2]{0,1:T(2,128)}, u32[]{:S(2)}) copy-start(s32[24,2]{0,1:T(2,128)} %param.8) | copy-start | bytes 580
  13.0 13.8 %collective-permute-start.1 = (bf16[512,1024]{1,0:T(8,128)(2,1)}, bf16[512,1024]{1,0:T(8,128)(2,1)S(1)}, u32[]{:S(2)}, u32[]{:S(2)}) collective-permute-start(bf16[512,1024]{1,0:T(8,128)(2,1)} %get-tuple-element.18), channel_id=1, source_target_pairs={{0,1},{1,0},{2,3},{3,2},{4,5},{5,4},{6,7},{7,6},{8,9},{9,8},{10,11... | collective-permute-start | bytes 3145736 | tf_op jit(solution)/shard_map/ppermute | solution.py:246
  13.4 16.2 %collective-permute-start.3 = (bf16[512,1024]{1,0:T(8,128)(2,1)}, bf16[512,1024]{1,0:T(8,128)(2,1)S(1)}, u32[]{:S(2)}, u32[]{:S(2)}) collective-permute-start(bf16[512,1024]{1,0:T(8,128)(2,1)} %get-tuple-element.20), channel_id=1, source_target_pairs={{0,1},{1,0},{2,3},{3,2},{4,5},{5,4},{6,7},{7,6},{8,9},{9,8},{10,11... | collective-permute-start | bytes 3145736 | tf_op jit(solution)/shard_map/ppermute | solution.py:246
  19.2 18.8 %copy-start.2 = (bf16[256,1024]{1,0:T(8,128)(2,1)S(1)}, bf16[256,1024]{1,0:T(8,128)(2,1)}, u32[]{:S(2)}) copy-start(bf16[256,1024]{1,0:T(8,128)(2,1)} %get-tuple-element.17) | copy-start | bytes 1572868
  20.7 16.4 %collective-permute-start.11 = (bf16[32,2048]{1,0:T(8,128)(2,1)}, bf16[32,2048]{1,0:T(8,128)(2,1)}, u32[]{:S(2)}, u32[]{:S(2)}) collective-permute-start(bf16[32,2048]{1,0:T(8,128)(2,1)} %get-tuple-element.29), channel_id=1, source_target_pairs={{0,24},{8,0},{16,8},{24,16},{1,25},{9,1},{17,9},{25,17},{2,26},{10... | collective-permute-start | bytes 393224 | tf_op jit(solution)/shard_map/ppermute | solution.py:255
  25.7 12.2 %collective-permute-start.13 = (bf16[32,2048]{1,0:T(8,128)(2,1)}, bf16[32,2048]{1,0:T(8,128)(2,1)S(1)}, u32[]{:S(2)}, u32[]{:S(2)}) collective-permute-start(bf16[32,2048]{1,0:T(8,128)(2,1)} %get-tuple-element.30), channel_id=1, source_target_pairs={{0,8},{8,16},{16,24},{24,0},{1,9},{9,17},{17,25},{25,1},{2,10},{10... | collective-permute-start | bytes 393224 | tf_op jit(solution)/shard_map/ppermute | solution.py:255
  25.7 22.8 %collective-permute-start.12 = (bf16[32,2048]{1,0:T(8,128)(2,1)}, bf16[32,2048]{1,0:T(8,128)(2,1)S(1)}, u32[]{:S(2)}, u32[]{:S(2)}) collective-permute-start(bf16[32,2048]{1,0:T(8,128)(2,1)} %get-tuple-element.31), channel_id=1, source_target_pairs={{0,16},{8,24},{16,0},{24,8},{1,17},{9,25},{17,1},{25,9},{2,18},{10... | collective-permute-start | bytes 393224 | tf_op jit(solution)/shard_map/ppermute | solution.py:255
  28.0 10.0 %collective-permute-start.2 = (bf16[256,1024]{1,0:T(8,128)(2,1)S(1)}, bf16[256,1024]{1,0:T(8,128)(2,1)}, u32[]{:S(2)}, u32[]{:S(2)}) collective-permute-start(bf16[256,1024]{1,0:T(8,128)(2,1)S(1)} %add_convert_fusion), channel_id=1, source_target_pairs={{0,4},{1,3},{2,6},{3,1},{4,0},{5,7},{6,2},{7,5},{8,12},{9,11},{10,... | collective-permute-start | bytes 1572872 | tf_op jit(solution)/shard_map/ppermute | solution.py:252
  29.6 1.0 copy-start.1
  36.6 9.4 %collective-permute-start.4 = (bf16[256,1024]{1,0:T(8,128)(2,1)}, bf16[256,1024]{1,0:T(8,128)(2,1)S(1)}, u32[]{:S(2)}, u32[]{:S(2)}) collective-permute-start(bf16[256,1024]{1,0:T(8,128)(2,1)} %get-tuple-element.22), channel_id=1, source_target_pairs={{0,4},{1,3},{2,6},{3,1},{4,0},{5,7},{6,2},{7,5},{8,12},{9,11},{10,... | collective-permute-start | bytes 1572872 | tf_op jit(solution)/shard_map/ppermute | solution.py:252
  47.0 20.5 %collective-permute-start.5 = (bf16[128,2048]{1,0:T(8,128)(2,1)S(1)}, bf16[128,2048]{1,0:T(8,128)(2,1)S(1)}, u32[]{:S(2)}, u32[]{:S(2)}) collective-permute-start(bf16[128,2048]{1,0:T(8,128)(2,1)S(1)} %pad_maximum_fusion), channel_id=1, source_target_pairs={{0,2},{1,5},{2,0},{3,7},{4,6},{5,1},{6,4},{7,3},{8,10},{9,13},{10,... | collective-permute-start | bytes 1572872 | tf_op jit(solution)/shard_map/ppermute | solution.py:252
  48.6 48.5 %copy-start = (bf16[128,1024]{1,0:T(8,128)(2,1)}, bf16[128,1024]{1,0:T(8,128)(2,1)S(1)}, u32[]{:S(2)}) copy-start(bf16[128,1024]{1,0:T(8,128)(2,1)S(1)} %pad_maximum_fusion.1.refs_0_) | copy-start | bytes 786436
  48.6 15.5 %collective-permute-start.16 = (bf16[128,1024]{1,0:T(8,128)(2,1)S(1)}, bf16[128,1024]{1,0:T(8,128)(2,1)S(1)}, u32[]{:S(2)}, u32[]{:S(2)}) collective-permute-start(bf16[128,1024]{1,0:T(8,128)(2,1)S(1)} %pad_maximum_fusion.1.refs_0_), channel_id=1, source_target_pairs={{0,6},{1,7},{2,4},{3,5},{4,2},{5,3},{6,0},{7,1},{8,14},{9,15},{10,... | collective-permute-start | bytes 786440 | tf_op jit(solution)/shard_map/ppermute | solution.py:252
  49.2 30.5 %copy-start.9 = (bf16[128,1024]{1,0:T(8,128)(2,1)}, bf16[128,1024]{1,0:T(8,128)(2,1)S(1)}, u32[]{:S(2)}) copy-start(bf16[128,1024]{1,0:T(8,128)(2,1)S(1)} %pad_maximum_fusion.2.refs_0_) | copy-start | bytes 786436
  49.2 16.8 %collective-permute-start.21 = (bf16[128,1024]{1,0:T(8,128)(2,1)S(1)}, bf16[128,1024]{1,0:T(8,128)(2,1)S(1)}, u32[]{:S(2)}, u32[]{:S(2)}) collective-permute-start(bf16[128,1024]{1,0:T(8,128)(2,1)S(1)} %pad_maximum_fusion.2.refs_0_), channel_id=1, source_target_pairs={{0,2},{1,5},{2,0},{3,7},{4,6},{5,1},{6,4},{7,3},{8,10},{9,13},{10,... | collective-permute-start | bytes 786440 | tf_op jit(solution)/shard_map/ppermute | solution.py:252
  50.8 18.6 %collective-permute-start.15 = (bf16[128,1024]{1,0:T(8,128)(2,1)S(1)}, bf16[128,1024]{1,0:T(8,128)(2,1)S(1)}, u32[]{:S(2)}, u32[]{:S(2)}) collective-permute-start(bf16[128,1024]{1,0:T(8,128)(2,1)S(1)} %pad_maximum_fusion.1.refs_0_), channel_id=1, source_target_pairs={{0,4},{1,3},{2,6},{3,1},{4,0},{5,7},{6,2},{7,5},{8,12},{9,11},{10,... | collective-permute-start | bytes 786440 | tf_op jit(solution)/shard_map/ppermute | solution.py:252
  52.3 23.0 %collective-permute-start.14 = (bf16[128,1024]{1,0:T(8,128)(2,1)S(1)}, bf16[128,1024]{1,0:T(8,128)(2,1)}, u32[]{:S(2)}, u32[]{:S(2)}) collective-permute-start(bf16[128,1024]{1,0:T(8,128)(2,1)S(1)} %pad_maximum_fusion.1.refs_0_), channel_id=1, source_target_pairs={{0,2},{1,5},{2,0},{3,7},{4,6},{5,1},{6,4},{7,3},{8,10},{9,13},{10,... | collective-permute-start | bytes 786440 | tf_op jit(solution)/shard_map/ppermute | solution.py:252
  64.2 33.0 %copy-start.3 = (bf16[128,1024]{1,0:T(8,128)(2,1)}, bf16[128,1024]{1,0:T(8,128)(2,1)S(1)}, u32[]{:S(2)}) copy-start(bf16[128,1024]{1,0:T(8,128)(2,1)S(1)} %collective-permute-done.16.refs_3_) | copy-start | bytes 786436
  64.2 14.5 %collective-permute-start.24 = (bf16[128,1024]{1,0:T(8,128)(2,1)S(1)}, bf16[128,1024]{1,0:T(8,128)(2,1)S(1)}, u32[]{:S(2)}, u32[]{:S(2)}) collective-permute-start(bf16[128,1024]{1,0:T(8,128)(2,1)S(1)} %pad_maximum_fusion.2.refs_0_), channel_id=1, source_target_pairs={{0,1},{1,0},{2,3},{3,2},{4,5},{5,4},{6,7},{7,6},{8,9},{9,8},{10,11... | collective-permute-start | bytes 786440 | tf_op jit(solution)/shard_map/ppermute | solution.py:246
  66.0 19.9 %copy-start.12 = (bf16[128,1024]{1,0:T(8,128)(2,1)}, bf16[128,1024]{1,0:T(8,128)(2,1)S(1)}, u32[]{:S(2)}) copy-start(bf16[128,1024]{1,0:T(8,128)(2,1)S(1)} %collective-permute-done.21.refs_1_) | copy-start | bytes 786436
  66.0 6.4 %collective-permute-start.22 = (bf16[128,1024]{1,0:T(8,128)(2,1)S(1)}, bf16[128,1024]{1,0:T(8,128)(2,1)S(1)}, u32[]{:S(2)}, u32[]{:S(2)}) collective-permute-start(bf16[128,1024]{1,0:T(8,128)(2,1)S(1)} %pad_maximum_fusion.2.refs_0_), channel_id=1, source_target_pairs={{0,4},{1,3},{2,6},{3,1},{4,0},{5,7},{6,2},{7,5},{8,12},{9,11},{10,... | collective-permute-start | bytes 786440 | tf_op jit(solution)/shard_map/ppermute | solution.py:252
  67.5 7.7 %collective-permute-start.23 = (bf16[128,1024]{1,0:T(8,128)(2,1)S(1)}, bf16[128,1024]{1,0:T(8,128)(2,1)S(1)}, u32[]{:S(2)}, u32[]{:S(2)}) collective-permute-start(bf16[128,1024]{1,0:T(8,128)(2,1)S(1)} %collective-permute-done.21.refs_1_), channel_id=1, source_target_pairs={{0,4},{1,3},{2,6},{3,1},{4,0},{5,7},{6,2},{7,5},{8,12},{9,11},{10,... | collective-permute-start | bytes 786440 | tf_op jit(solution)/shard_map/ppermute | solution.py:252
  69.4 27.8 %copy-start.4 = (bf16[128,1024]{1,0:T(8,128)(2,1)}, bf16[128,1024]{1,0:T(8,128)(2,1)S(1)}, u32[]{:S(2)}) copy-start(bf16[128,1024]{1,0:T(8,128)(2,1)S(1)} %collective-permute-done.15.refs_2_) | copy-start | bytes 786436
  69.4 9.7 %collective-permute-start.26 = (bf16[128,1024]{1,0:T(8,128)(2,1)S(1)}, bf16[128,1024]{1,0:T(8,128)(2,1)S(1)}, u32[]{:S(2)}, u32[]{:S(2)}) collective-permute-start(bf16[128,1024]{1,0:T(8,128)(2,1)S(1)} %collective-permute-done.21.refs_1_), channel_id=1, source_target_pairs={{0,1},{1,0},{2,3},{3,2},{4,5},{5,4},{6,7},{7,6},{8,9},{9,8},{10,11... | collective-permute-start | bytes 786440 | tf_op jit(solution)/shard_map/ppermute | solution.py:246
  72.4 13.6 %copy-start.14 = (bf16[128,1024]{1,0:T(8,128)(2,1)}, bf16[128,1024]{1,0:T(8,128)(2,1)S(1)}, u32[]{:S(2)}) copy-start(bf16[128,1024]{1,0:T(8,128)(2,1)S(1)} %collective-permute-done.22.refs_2_) | copy-start | bytes 786436
  72.4 6.7 %collective-permute-start.25 = (bf16[128,1024]{1,0:T(8,128)(2,1)S(1)}, bf16[128,1024]{1,0:T(8,128)(2,1)S(1)}, u32[]{:S(2)}, u32[]{:S(2)}) collective-permute-start(bf16[128,1024]{1,0:T(8,128)(2,1)S(1)} %collective-permute-done.22.refs_2_), channel_id=1, source_target_pairs={{0,1},{1,0},{2,3},{3,2},{4,5},{5,4},{6,7},{7,6},{8,9},{9,8},{10,11... | collective-permute-start | bytes 786440 | tf_op jit(solution)/shard_map/ppermute | solution.py:246
  75.2 11.4 %copy-start.15 = (bf16[128,1024]{1,0:T(8,128)(2,1)}, bf16[128,1024]{1,0:T(8,128)(2,1)S(1)}, u32[]{:S(2)}) copy-start(bf16[128,1024]{1,0:T(8,128)(2,1)S(1)} %collective-permute-done.23.refs_3_) | copy-start | bytes 786436
  75.2 4.5 %collective-permute-start.27 = (bf16[128,1024]{1,0:T(8,128)(2,1)S(1)}, bf16[128,1024]{1,0:T(8,128)(2,1)S(1)}, u32[]{:S(2)}, u32[]{:S(2)}) collective-permute-start(bf16[128,1024]{1,0:T(8,128)(2,1)S(1)} %collective-permute-done.23.refs_3_), channel_id=1, source_target_pairs={{0,1},{1,0},{2,3},{3,2},{4,5},{5,4},{6,7},{7,6},{8,9},{9,8},{10,11... | collective-permute-start | bytes 786440 | tf_op jit(solution)/shard_map/ppermute | solution.py:246
  75.2 8.2 %collective-permute-start.6 = (bf16[32,2048]{1,0:T(8,128)(2,1)S(1)}, bf16[32,2048]{1,0:T(8,128)(2,1)S(1)}, u32[]{:S(2)}, u32[]{:S(2)}) collective-permute-start(bf16[32,2048]{1,0:T(8,128)(2,1)S(1)} %get-tuple-element.33), channel_id=1, source_target_pairs={{0,8},{8,16},{16,24},{24,0},{1,9},{9,17},{17,25},{25,1},{2,10},{10... | collective-permute-start | bytes 393224 | tf_op jit(solution)/shard_map/ppermute | solution.py:255
  78.7 7.3 %copy-start.13 = (bf16[128,1024]{1,0:T(8,128)(2,1)}, bf16[128,1024]{1,0:T(8,128)(2,1)S(1)}, u32[]{:S(2)}) copy-start(bf16[128,1024]{1,0:T(8,128)(2,1)S(1)} %collective-permute-done.24.refs_4_) | copy-start | bytes 786436
  78.7 7.3 %collective-permute-start.8 = (bf16[32,2048]{1,0:T(8,128)(2,1)S(1)}, bf16[32,2048]{1,0:T(8,128)(2,1)}, u32[]{:S(2)}, u32[]{:S(2)}) collective-permute-start(bf16[32,2048]{1,0:T(8,128)(2,1)S(1)} %get-tuple-element.34), channel_id=1, source_target_pairs={{0,24},{8,0},{16,8},{24,16},{1,25},{9,1},{17,9},{25,17},{2,26},{10... | collective-permute-start | bytes 393224 | tf_op jit(solution)/shard_map/ppermute | solution.py:255
  79.1 7.4 %copy-start.17 = (bf16[128,1024]{1,0:T(8,128)(2,1)}, bf16[128,1024]{1,0:T(8,128)(2,1)S(1)}, u32[]{:S(2)}) copy-start(bf16[128,1024]{1,0:T(8,128)(2,1)S(1)} %collective-permute-done.25.refs_5_) | copy-start | bytes 786436
  79.1 18.0 %collective-permute-start.17 = (bf16[128,1024]{1,0:T(8,128)(2,1)S(1)}, bf16[128,1024]{1,0:T(8,128)(2,1)S(1)}, u32[]{:S(2)}, u32[]{:S(2)}) collective-permute-start(bf16[128,1024]{1,0:T(8,128)(2,1)S(1)} %pad_maximum_fusion.1.refs_0_), channel_id=1, source_target_pairs={{0,1},{1,0},{2,3},{3,2},{4,5},{5,4},{6,7},{7,6},{8,9},{9,8},{10,11... | collective-permute-start | bytes 786440 | tf_op jit(solution)/shard_map/ppermute | solution.py:246
  79.2 7.4 %copy-start.16 = (bf16[128,1024]{1,0:T(8,128)(2,1)}, bf16[128,1024]{1,0:T(8,128)(2,1)S(1)}, u32[]{:S(2)}) copy-start(bf16[128,1024]{1,0:T(8,128)(2,1)S(1)} %collective-permute-done.26.refs_6_) | copy-start | bytes 786436
  79.2 17.9 %collective-permute-start.20 = (bf16[128,1024]{1,0:T(8,128)(2,1)S(1)}, bf16[128,1024]{1,0:T(8,128)(2,1)S(1)}, u32[]{:S(2)}, u32[]{:S(2)}) collective-permute-start(bf16[128,1024]{1,0:T(8,128)(2,1)S(1)} %collective-permute-done.16.refs_3_), channel_id=1, source_target_pairs={{0,1},{1,0},{2,3},{3,2},{4,5},{5,4},{6,7},{7,6},{8,9},{9,8},{10,11... | collective-permute-start | bytes 786440 | tf_op jit(solution)/shard_map/ppermute | solution.py:246
  79.7 6.9 %copy-start.18 = (bf16[128,1024]{1,0:T(8,128)(2,1)}, bf16[128,1024]{1,0:T(8,128)(2,1)S(1)}, u32[]{:S(2)}) copy-start(bf16[128,1024]{1,0:T(8,128)(2,1)S(1)} %collective-permute-done.27.refs_7_) | copy-start | bytes 786436
  79.7 17.5 %collective-permute-start.18 = (bf16[128,1024]{1,0:T(8,128)(2,1)S(1)}, bf16[128,1024]{1,0:T(8,128)(2,1)S(1)}, u32[]{:S(2)}, u32[]{:S(2)}) collective-permute-start(bf16[128,1024]{1,0:T(8,128)(2,1)S(1)} %collective-permute-done.15.refs_2_), channel_id=1, source_target_pairs={{0,1},{1,0},{2,3},{3,2},{4,5},{5,4},{6,7},{7,6},{8,9},{9,8},{10,11... | collective-permute-start | bytes 786440 | tf_op jit(solution)/shard_map/ppermute | solution.py:246
  83.5 13.7 %collective-permute-start.19 = (bf16[128,1024]{1,0:T(8,128)(2,1)}, bf16[128,1024]{1,0:T(8,128)(2,1)S(1)}, u32[]{:S(2)}, u32[]{:S(2)}) collective-permute-start(bf16[128,1024]{1,0:T(8,128)(2,1)} %collective-permute-done.14.refs_1_), channel_id=1, source_target_pairs={{0,1},{1,0},{2,3},{3,2},{4,5},{5,4},{6,7},{7,6},{8,9},{9,8},{10,11... | collective-permute-start | bytes 786440 | tf_op jit(solution)/shard_map/ppermute | solution.py:246
  85.9 9.9 %collective-permute-start.7 = (bf16[32,2048]{1,0:T(8,128)(2,1)S(1)}, bf16[32,2048]{1,0:T(8,128)(2,1)S(1)}, u32[]{:S(2)}, u32[]{:S(2)}) collective-permute-start(bf16[32,2048]{1,0:T(8,128)(2,1)S(1)} %get-tuple-element.35), channel_id=1, source_target_pairs={{0,16},{8,24},{16,0},{24,8},{1,17},{9,25},{17,1},{25,9},{2,18},{10... | collective-permute-start | bytes 393224 | tf_op jit(solution)/shard_map/ppermute | solution.py:255
  97.0 10.4 %collective-permute-start.9 = (bf16[24,2048]{1,0:T(8,128)(2,1)S(1)}, bf16[24,2048]{1,0:T(8,128)(2,1)S(1)}, u32[]{:S(2)}, u32[]{:S(2)}) collective-permute-start(bf16[24,2048]{1,0:T(8,128)(2,1)S(1)} %slice.158), channel_id=1, source_target_pairs={{0,1},{1,0},{2,3},{3,2},{4,5},{5,4},{6,7},{7,6},{8,9},{9,8},{10,11... | collective-permute-start | bytes 294920 | tf_op jit(solution)/shard_map/ppermute | solution.py:246
  97.1 0.7 copy-start.5
  97.1 0.8 copy-start.6
  97.1 0.9 copy-start.7
  97.2 1.0 copy-start.8

commit v2 on v1

v2 whole, which is shorter than its diff:
```python
import jax
import jax.numpy as jnp
from jax import lax
from jax.experimental import pallas as pl
from jax.experimental.pallas import tpu as pltpu
from jax.sharding import PartitionSpec as P


PARTS = 2


def kernel_params(rows):
    mebibytes = 40 if rows <= 512 else 60
    return pltpu.CompilerParams(vmem_limit_bytes=mebibytes * 1024 * 1024)


DIRECT = (False, True)


def block_width(width, limit):
    block = min(width, limit)
    while width % block:
        block //= 2
    return block


def times_transposed(left, right):
    return lax.dot_general(left, right, (((1,), (1,)), ((), ())), preferred_element_type=jnp.float32)


def rows_inner(left, right):
    return lax.dot_general(left, right, (((0,), (0,)), ((), ())), preferred_element_type=jnp.float32)


def reverse_bits(value, count):
    return sum(((value >> b) & 1) << (count - 1 - b) for b in range(count))


def core_of(place, shards):
    return lax.rem(place[0], shards) & 1


def chip_of(place, shards, v, plane):
    count = len(plane)
    shard = lax.rem(place[0], shards)
    core = shard & 1
    masks = [sum(bits[b] for b in range(count) if (v >> b) & 1) for bits in (plane, plane[::-1])]
    return (shard ^ jnp.where(core == 0, masks[0], masks[1])) - core


def swiglu_rows(place, shards, v, source_ref, grads_ref, groups, capacity):
    expert = lax.div(place[0], shards)
    first = v * groups * 2 * capacity

    def body(n, carry):
        source = (lax.rem(n, 2) * groups + lax.rem(expert + lax.div(n, 2), groups)) * capacity
        rows = pl.ds(pl.multiple_of(first + source, capacity), capacity)
        to = pl.ds(pl.multiple_of(first + n * capacity, capacity), capacity)
        a = source_ref[0, rows, :].astype(jnp.float32)
        b = source_ref[1, rows, :].astype(jnp.float32)
        g = source_ref[2, rows, :].astype(jnp.float32)
        sig = 0.5 + 0.5 * jnp.tanh(0.5 * a)
        gs = g * sig
        grads_ref[0, to, :] = (gs * b * (1.0 + a * (1.0 - sig))).astype(jnp.bfloat16)
        grads_ref[1, to, :] = (gs * a).astype(jnp.bfloat16)
        return carry

    lax.fori_loop(0, groups * 2, body, 0)


def dgrad_cost(rows, units, width, extra):
    return pl.CostEstimate(
        flops=4 * rows * units * width, transcendentals=0,
        bytes_accessed=4 * rows * units + 4 * units * width + 2 * rows * width + extra,
    )


def weight_loads(color, wg_ref, wu_ref, weights_ref, sems, block):
    width = weights_ref.shape[1]
    copies = []
    for step in range(width // block):
        first = pl.multiple_of(color * width + step * block, block)
        for n, ref in enumerate((wg_ref, wu_ref)):
            copies.append(
                pltpu.make_async_copy(
                    ref.at[pl.ds(first, block), :],
                    weights_ref.at[n, pl.ds(step * block, block), :],
                    sems.at[2 * step + n],
                )
            )
    return copies


def block_product(grads_ref, weights_ref, loads, step, block):
    acc = None
    for n in range(2):
        loads[2 * step + n].wait()
        for copy in loads[2 * step + n + 2 : 2 * step + n + 3]:
            copy.start()
        term = times_transposed(grads_ref[n], weights_ref[n, step * block : (step + 1) * block, :])
        acc = term if acc is None else acc + term
    return acc


def dgrad_other(place, shards, sources, weight_gate, weight_up, plane, groups, capacity):
    rows, units = sources[0].shape
    width = weight_gate.shape[0] // 2
    block = block_width(width, 512)
    steps = width // block
    count = len(plane)
    chips = 1 << count
    chip_rows = rows // chips

    def kernel(place_ref, *refs):
        source_refs, (wg_ref, wu_ref, gate_out, up_out, out_ref) = refs[:3], refs[3:8]
        source_ref, grads_ref, weights_ref, stage_ref = refs[8:12]
        source_sems, weight_sems, grad_sems, out_sems = refs[12:]
        loads = []
        for v in range(chips):
            chip = chip_of(place_ref, shards, v, plane)
            first = pl.multiple_of(chip * (groups * capacity), chip_rows)
            here = pl.ds(v * chip_rows, chip_rows)
            for n, ref in enumerate(source_refs):
                loads.append(
                    pltpu.make_async_copy(
                        ref.at[pl.ds(first, chip_rows), :],
                        source_ref.at[n, here, :],
                        source_sems.at[3 * v + n],
                    )
                )
        weights = weight_loads(
            1 - core_of(place_ref, shards), wg_ref, wu_ref, weights_ref, weight_sems, block
        )
        for copy in loads:
            copy.start()
        for v in range(chips):
            for copy in loads[3 * v : 3 * v + 3]:
                copy.wait()
            if v == chips - 1:
                for copy in weights[:2]:
                    copy.start()
            swiglu_rows(place_ref, shards, v, source_ref, grads_ref, groups, capacity)
        stores = [
            pltpu.make_async_copy(grads_ref.at[n], out, grad_sems.at[n])
            for n, out in enumerate((gate_out, up_out))
        ]
        for copy in stores:
            copy.start()
        outs = []
        for step in range(steps):
            acc = block_product(grads_ref, weights_ref, weights, step, block).astype(jnp.bfloat16)
            slot = step % 2
            if step >= 2:
                outs[step - 2].wait()
            for v in range(chips):
                u = reverse_bits(v, count)
                stage_ref[slot, v * chip_rows : (v + 1) * chip_rows, :] = acc[
                    u * chip_rows : (u + 1) * chip_rows, :
                ]
            outs.append(
                pltpu.make_async_copy(
                    stage_ref.at[slot], out_ref.at[:, pl.ds(step * block, block)], out_sems.at[slot]
                )
            )
            outs[-1].start()
        for copy in stores + outs[-2:]:
            copy.wait()

    anywhere = pl.BlockSpec(memory_space=pl.ANY)
    grads = jax.ShapeDtypeStruct((rows, units), jnp.bfloat16)
    return pl.pallas_call(
        kernel,
        name="dgrad_other",
        in_specs=[pl.BlockSpec(memory_space=pltpu.SMEM)] + [anywhere] * 5,
        out_specs=[anywhere] * 3,
        scratch_shapes=[
            pltpu.VMEM((3, rows, units), jnp.bfloat16),
            pltpu.VMEM((2, rows, units), jnp.bfloat16),
            pltpu.VMEM((2, width, units), jnp.bfloat16),
            pltpu.VMEM((2, rows, block), jnp.bfloat16),
            pltpu.SemaphoreType.DMA((3 * chips,)),
            pltpu.SemaphoreType.DMA((2 * steps,)),
            pltpu.SemaphoreType.DMA((2,)),
            pltpu.SemaphoreType.DMA((2,)),
        ],
        out_shape=[grads, grads, jax.ShapeDtypeStruct((rows, width), jnp.bfloat16)],
        compiler_params=kernel_params(rows),
        cost_estimate=dgrad_cost(rows, units, width, 6 * rows * units),
    )(place, *[in_hbm(array) for array in (*sources, weight_gate, weight_up)])


def dgrad_own(place, shards, gate_rows, up_rows, weight_gate, weight_up, came):
    rows, units = gate_rows.shape
    width = weight_gate.shape[0] // 2
    block = block_width(width, 512)
    steps = width // block
    middle = rows // 2

    def kernel(place_ref, gate_ref, up_ref, wg_ref, wu_ref, came_ref, *refs):
        high_ref, low_ref, grads_ref, weights_ref, added_ref, stage_ref = refs[:6]
        grad_sems, weight_sems, added_sems, out_sems = refs[6:]
        grads = [
            pltpu.make_async_copy(ref, grads_ref.at[n], grad_sems.at[n])
            for n, ref in enumerate((gate_ref, up_ref))
        ]
        weights = weight_loads(
            core_of(place_ref, shards), wg_ref, wu_ref, weights_ref, weight_sems, block
        )
        added = [
            pltpu.make_async_copy(
                came_ref.at[:, pl.ds(step * block, block)], added_ref.at[step % 2], added_sems.at[step % 2]
            )
            for step in range(steps)
        ]
        for copy in [grads[0], weights[0], grads[1], weights[1], *added[:2]]:
            copy.start()
        for copy in grads:
            copy.wait()
        outs = []
        for step in range(steps):
            slot = step % 2
            acc = block_product(grads_ref, weights_ref, weights, step, block)
            added[step].wait()
            if step >= 2:
                for copy in outs[step - 2]:
                    copy.wait()
            stage_ref[slot] = (acc + added_ref[slot].astype(jnp.float32)).astype(jnp.bfloat16)
            if step + 2 < steps:
                added[step + 2].start()
            columns = pl.ds(step * block, block)
            outs.append([
                pltpu.make_async_copy(
                    stage_ref.at[slot, pl.ds(part * middle, middle), :],
                    ref.at[:, columns],
                    out_sems.at[2 * slot + part],
                )
                for part, ref in enumerate((low_ref, high_ref))
            ])
            for copy in outs[-1]:
                copy.start()
        for copies in outs[-2:]:
            for copy in copies:
                copy.wait()

    anywhere = pl.BlockSpec(memory_space=pl.ANY)
    return pl.pallas_call(
        kernel,
        name="dgrad_own",
        in_specs=[pl.BlockSpec(memory_space=pltpu.SMEM)] + [anywhere] * 5,
        out_specs=[anywhere] * 2,
        scratch_shapes=[
            pltpu.VMEM((2, rows, units), jnp.bfloat16),
            pltpu.VMEM((2, width, units), jnp.bfloat16),
            pltpu.VMEM((2, rows, block), jnp.bfloat16),
            pltpu.VMEM((2, rows, block), jnp.bfloat16),
            pltpu.SemaphoreType.DMA((2,)),
            pltpu.SemaphoreType.DMA((2 * steps,)),
            pltpu.SemaphoreType.DMA((2,)),
            pltpu.SemaphoreType.DMA((4,)),
        ],
        out_shape=[jax.ShapeDtypeStruct((middle, width), jnp.bfloat16)] * 2,
        compiler_params=kernel_params(rows),
        cost_estimate=dgrad_cost(rows, units, width, 2 * rows * width),
    )(place, gate_rows, up_rows, in_hbm(weight_gate), in_hbm(weight_up), came)


def in_hbm(value):
    return pltpu.with_memory_space_constraint(value, pltpu.HBM)


def wgrad(place, shards, own_pieces, other_pieces, gate_rows, up_rows, part, parts, into):
    rows, units = gate_rows.shape
    pieces = len(own_pieces)
    piece_rows, width = own_pieces[0].shape
    block = block_width(width, 512)
    steps = width // block
    slots = 4

    def kernel(place_ref, *refs):
        gate_ref, up_ref = refs[2 * pieces : 2 * pieces + 2]
        gate_out, up_out, left_ref, grads_ref, slot_ref, in_sems, out_sems = refs[-7:]
        core = core_of(place_ref, shards)

        def load(n, source, target):
            return pltpu.make_async_copy(source, target, in_sems.at[n])

        grads_in = [load(n, ref, grads_ref.at[n]) for n, ref in enumerate((gate_ref, up_ref))]
        left_in = [
            load(2 + n, ref, left_ref.at[n // pieces, pl.ds(n % pieces * piece_rows, piece_rows), :])
            for n, ref in enumerate(refs[: 2 * pieces])
        ]
        for copy in grads_in[:1] + left_in[:pieces]:
            copy.start()
        stores = []
        for color in range(2):
            for copy in left_in[color * pieces : (color + 1) * pieces]:
                copy.wait()
            where = jnp.where(color == 0, core, 1 - core) * parts + part
            for step in range(steps):
                for n, out in enumerate((gate_out, up_out)):
                    if color == 0 and step == 0:
                        grads_in[n].wait()
                        if n == 0:
                            for copy in grads_in[1:] + left_in[pieces:]:
                                copy.start()
                    slot = len(stores) % slots
                    if len(stores) >= slots:
                        stores[-slots].wait()
                    slot_ref[slot] = rows_inner(
                        left_ref[color, :, step * block : (step + 1) * block], grads_ref[n]
                    )
                    first = pl.multiple_of((where * steps + step) * block, block)
                    stores.append(
                        pltpu.make_async_copy(
                            slot_ref.at[slot], out.at[pl.ds(first, block), :], out_sems.at[slot]
                        )
                    )
                    stores[-1].start()
        for copy in stores[-slots:]:
            copy.wait()

    operands = (place, *own_pieces, *other_pieces, gate_rows, up_rows, *into)
    anywhere = pl.BlockSpec(memory_space=pl.ANY)
    return pl.pallas_call(
        kernel,
        in_specs=[pl.BlockSpec(memory_space=pltpu.SMEM)] + [anywhere] * (len(operands) - 1),
        out_specs=[anywhere] * 2,
        scratch_shapes=[
            pltpu.VMEM((2, rows, width), jnp.bfloat16),
            pltpu.VMEM((2, rows, units), jnp.bfloat16),
            pltpu.VMEM((slots, block, units), jnp.float32),
            pltpu.SemaphoreType.DMA((2 + 2 * pieces,)),
            pltpu.SemaphoreType.DMA((slots,)),
        ],
        out_shape=[jax.ShapeDtypeStruct((2 * parts * width, units), jnp.float32)] * 2,
        input_output_aliases={len(operands) - len(into) + n: n for n in range(len(into))},
        compiler_params=kernel_params(rows),
        cost_estimate=pl.CostEstimate(
            flops=8 * rows * units * width, transcendentals=0,
            bytes_accessed=4 * rows * units + 4 * rows * width + 16 * units * width,
        ),
    )(*operands)


def total(terms):
    value = terms[0].astype(jnp.float32)
    for term in terms[1:]:
        value = value + term.astype(jnp.float32)
    return value.astype(jnp.bfloat16)


def on_device(tokens, expert_ids, weight_gate, weight_up, gate_pre, up_pre, hidden_grad):
    groups = lax.axis_size("expert")
    shards = lax.axis_size("shard")
    expert = lax.axis_index("expert")
    shard = lax.axis_index("shard")
    token_count, model_width = tokens.shape
    capacity = gate_pre.shape[1] // (groups * shards)
    half = model_width // 2
    bits = [1 << b for b in range(shards.bit_length() - 1)]
    assert 1 << len(bits) == shards
    plane = bits[1:]
    count = len(plane)
    core = shard & 1
    place = (expert * shards + shard).astype(jnp.int32).reshape(1)

    def over_core(value):
        return lax.ppermute(value, "shard", [(i, i ^ 1) for i in range(shards)])

    def over_plane(value, v):
        masks = [
            sum(bits[b] for b in range(count) if (v >> b) & 1) for bits in (plane, plane[::-1])
        ]
        return lax.ppermute(value, "shard", [(i, i ^ masks[i & 1]) for i in range(shards)])

    def over_expert(value, step):
        return lax.ppermute(value, "expert", [(i, (i + step) % groups) for i in range(groups)])

    def by_core(first, second):
        return jnp.where(core == 0, first, second)

    peer_tokens = over_core(tokens)
    peer_ids = over_core(expert_ids)
    both = jnp.concatenate([tokens, peer_tokens], axis=0)
    both = by_core(both[:, :half], both[:, half:])
    both_ids = jnp.concatenate([expert_ids, peer_ids], axis=0)

    relative = lax.rem(expert - both_ids + groups, groups)
    shape = (2 * token_count, groups * 2 * capacity)
    column = lax.broadcasted_iota(jnp.int32, shape, 1)
    token = lax.broadcasted_iota(jnp.int32, shape, 0)
    distance = column // (2 * capacity)
    named = jnp.any(relative[:, :, None] == distance[:, None, :], axis=1)
    named = named & (token // token_count ^ core == column // capacity % 2)
    named = named.astype(jnp.bfloat16)
    square = (2 * token_count, 2 * token_count)
    lower = lax.broadcasted_iota(jnp.int32, square, 0) > lax.broadcasted_iota(jnp.int32, square, 1)
    earlier = lax.dot_general(
        lower.astype(jnp.bfloat16), named, (((1,), (0,)), ((), ())), preferred_element_type=jnp.float32
    )
    selection = jnp.where(earlier == (column % capacity).astype(jnp.float32), named, 0)

    outgoing = rows_inner(selection, both).astype(jnp.bfloat16)
    outgoing = outgoing.reshape(groups, 2 * capacity, half)
    arrived = [outgoing[0]]
    for k in range(1, groups):
        arrived.append(over_expert(outgoing[k], groups - k))

    weights = (weight_gate[0], weight_up[0])
    gate_rows, up_rows, away = dgrad_other(
        place, shards, (gate_pre[0], up_pre[0], hidden_grad[0]), *weights, plane, groups, capacity
    )
    came = over_core(away)
    high, low = dgrad_own(place, shards, gate_rows, up_rows, *weights, came)
    terms = [low]
    for b in range(count)[::-1]:
        if b < count - 1:
            middle = terms[0].shape[0] // 2
            high = total([t[middle:] for t in terms])
            terms = [t[:middle] for t in terms]
        terms.append(over_plane(high, 1 << b))
    summed = total(terms)

    masks = range(1 << count)
    grads = ()
    part_width = half // PARTS
    for part in range(PARTS):
        columns = slice(part * part_width, (part + 1) * part_width)
        held = {0: jnp.concatenate([rows[:, columns] for rows in arrived], axis=0)}
        for v in masks[1:]:
            bit = v if DIRECT[part] else 1 << v.bit_length() - 1
            held[v] = over_plane(held[v ^ bit], bit)
        swapped = {}
        for v in masks:
            swapped[v] = over_core(held[v])
        grads = wgrad(
            place,
            shards,
            [held[v] for v in masks],
            [swapped[reverse_bits(v, count)] for v in masks],
            gate_rows,
            up_rows,
            part,
            PARTS,
            grads,
        )
    gate_wgrad, up_wgrad = grads

    blocks = summed.reshape(groups, 2 * capacity, half)
    back = [blocks[0]]
    for k in range(1, groups):
        back.append(over_expert(blocks[k], k))
    combined = lax.dot_general(
        selection, jnp.concatenate(back, axis=0), (((1,), (0,)), ((), ())),
        preferred_element_type=jnp.float32,
    ).astype(jnp.bfloat16)
    kept = combined[:token_count]
    got = over_core(combined[token_count:])
    token_grad = jnp.concatenate([by_core(kept, got), by_core(got, kept)], axis=1)
    return (token_grad, gate_wgrad[None], up_wgrad[None])


def solution(mesh):
    placed = (
        P(("expert", "shard"), None),
        P(("expert", "shard"), None),
        P("expert", None, "shard"),
        P("expert", None, "shard"),
        P("expert", None, "shard"),
        P("expert", None, "shard"),
        P("expert", None, "shard"),
    )

    return jax.shard_map(
        on_device,
        mesh=mesh,
        in_specs=placed,
        out_specs=(
            P(("expert", "shard"), None),
            P("expert", None, "shard"),
            P("expert", None, "shard"),
        ),
        check_vma=False,
    )
```

time: 110 us -> 99.2 us (0.902); the launches traced: 108 us -> 99 us
  Pallas kernels: 41.8 us -> 33.4 us
  waiting for transfers between devices: 32 us -> 38 us
  other arithmetic: 5.69 us -> 1.33 us
  local copies, waits for them, and re-layouts: 3.66 us -> 0.15 us
  starting transfers between devices: 22.2 us -> 24.4 us
    ppermute x6, waiting for transfers between devices: 6.2 us -> 15.3 us  [over_expert(): lax.ppermute(value, 'expert', [(i, (i + step) % groups) for i in range(gr...]
    pallas_call x5 -> x4, Pallas kernels: 41.8 us -> 33.4 us  [the longest x2 14.6 us: wgrad(): pl.pallas_call(kernel, in_specs=[pl.BlockSpec(memory_space=pltpu.SMEM)] +...]
    ppermute x9 -> x8, waiting for transfers between devices: 25.8 us -> 19.4 us  [over_plane(): lax.ppermute(value, 'shard', [(i, i ^ masks[i & 1]) for i in range(shards)])]
    convert_element_type x4 -> x2, other arithmetic: 4.65 us -> 0.36 us  [total(): return value.astype(jnp.bfloat16)]
    ppermute x13 -> x12, waiting for transfers between devices: 0.03 us -> 3.27 us  [over_core(): return lax.ppermute(value, 'shard', [(i, i ^ 1) for i in range(shards)])]
    unnamed x39 -> x5, local copies, waits for them, and re-layouts: 1.97 us -> 0.02 us
    ppermute x9 -> x8, starting transfers between devices: 9.83 us -> 11.5 us  [over_plane(): lax.ppermute(value, 'shard', [(i, i ^ masks[i & 1]) for i in range(shards)])]
    ppermute x13 -> x12, starting transfers between devices: 1.88 us -> 3.04 us  [over_core(): return lax.ppermute(value, 'shard', [(i, i ^ 1) for i in range(shards)])]
  transfers between devices with their start and end apart: 28 -> 26, of which waited for: 7 -> 11; matrix products, arithmetic and copies ran while one was open for 8% -> 2% of each run, Pallas kernels for 39% -> 26%
where the time goes in v2:
time: 99.2 us; the launch traced here: 99 us
  waiting for transfers between devices  38 us (38%)
  Pallas kernels  33.4 us (34%)
  starting transfers between devices  24.4 us (25%)
  other arithmetic  1.33 us (1%)
    ppermute x8, waiting for transfers between devices, over_plane(): lax.ppermute(value, 'shard', [(i, i ^ masks[i & 1]) for i in range(shards)])  19.4 us
    ppermute x6, waiting for transfers between devices, over_expert(): lax.ppermute(value, 'expert', [(i, (i + step) % groups) for i in range(gr...  15.3 us
    pallas_call x2, Pallas kernels, wgrad(): pl.pallas_call(kernel, in_specs=[pl.BlockSpec(memory_space=pltpu.SMEM)] +...  14.6 us
    ppermute x8, starting transfers between devices, over_plane(): lax.ppermute(value, 'shard', [(i, i ^ masks[i & 1]) for i in range(shards)])  11.5 us
    pallas_call x1, Pallas kernels, dgrad_other(): pl.pallas_call(kernel, name='dgrad_other', in_specs=[pl.BlockSpec(memory_...  10.6 us
    ppermute x6, starting transfers between devices, over_expert(): lax.ppermute(value, 'expert', [(i, (i + step) % groups) for i in range(gr...  9.91 us
    pallas_call x1, Pallas kernels, dgrad_own(): pl.pallas_call(kernel, name='dgrad_own', in_specs=[pl.BlockSpec(memory_sp...  8.11 us
    ppermute x12, waiting for transfers between devices, over_core(): return lax.ppermute(value, 'shard', [(i, i ^ 1) for i in range(shards)])  3.27 us
  transfers between devices with their start and end apart: 26, of which 11 were waited for; matrix products, arithmetic and copies ran while one was open for 2% of the time, Pallas kernels for 26%

profile of v2, /device:TPU:0, one launch (start us, length us, event | category | flops | bytes accessed | tf_op | source)
XLA Modules:
  0.0 99.0 jit_solution(9384623553637146271)
XLA Ops:
  0.7 0.6 collective-permute-start
  1.2 0.1 collective-permute-start.8
  1.3 10.6 %dgrad_other.1 = (bf16[512,1024]{1,0:T(8,128)(2,1)S(1)}, bf16[512,1024]{1,0:T(8,128)(2,1)S(1)}, bf16[512,2048]{1,0:T(8,128)(2,1)}) custom-call(s32[1]{0:T(128)} %bitcast.place_ref, bf16[512,1024]{1,0:T(8,128)(2,1)} %bitcast.16, bf16[512,1024]{1,0:T(8,128)(2,1)} %bitcast.17, bf16[512,1024]{1,0:T(8,128)(2,1)} %bitcast.18, bf16[4096,1024]{1,0:T(8,128)(2,1)} %bitcast.10, ...), custom_call_target="tpu_custom_call" | custom-call | flops 4294967296 | bytes 15728640 | tf_op jit(solution)/shard_map/dgrad_other/pallas_call | solution.py:171
  11.9 0.5 collective-permute-start.1
  12.6 0.1 compare_select_fusion
  12.7 0.1 compare_reduce_fusion
  12.7 0.2 fusion
  13.0 0.3 convolution_convert_fusion
  13.3 3.2 %collective-permute-done.1.came_ref = bf16[512,2048]{1,0:T(8,128)(2,1)} collective-permute-done((bf16[512,2048]{1,0:T(8,128)(2,1)}, bf16[512,2048]{1,0:T(8,128)(2,1)}, u32[]{:S(2)}, u32[]{:S(2)}) %collective-permute-start.1) | collective-permute-done | bytes 2097184 | tf_op jit(solution)/shard_map/ppermute | solution.py:368
  16.5 8.1 %dgrad_own.1 = (bf16[256,2048]{1,0:T(8,128)(2,1)S(1)}, bf16[256,2048]{1,0:T(8,128)(2,1)S(1)}) custom-call(s32[1]{0:T(128)} %bitcast.place_ref, bf16[512,1024]{1,0:T(8,128)(2,1)S(1)} %get-tuple-element.12.gate_ref.refs_8_, bf16[512,1024]{1,0:T(8,128)(2,1)S(1)} %get-tuple-element.13.up_ref.refs_9_, bf16[4096,1024]{1,0:T(8,128)(2,1)} %bitcast.11, ...), custom_call_target="tpu_custom_call" | custom-call | flops 4294967296 | bytes 14680064 | tf_op jit(solution)/shard_map/dgrad_own/pallas_call | solution.py:246
  24.7 2.9 %collective-permute-start.2 = (bf16[256,2048]{1,0:T(8,128)(2,1)S(1)}, bf16[256,2048]{1,0:T(8,128)(2,1)S(1)}, u32[]{:S(2)}, u32[]{:S(2)}) collective-permute-start(bf16[256,2048]{1,0:T(8,128)(2,1)S(1)} %get-tuple-element.16), channel_id=1, source_target_pairs={{0,4},{1,3},{2,6},{3,1},{4,0},{5,7},{6,2},{7,5},{8,12},{9,11},{10,... | collective-permute-start | bytes 3145736 | tf_op jit(solution)/shard_map/ppermute | solution.py:374
  27.6 3.6 %collective-permute-start.9 = (bf16[32,2048]{1,0:T(8,128)(2,1)S(1)}, bf16[32,2048]{1,0:T(8,128)(2,1)S(1)}, u32[]{:S(2)}, u32[]{:S(2)}) collective-permute-start(bf16[32,2048]{1,0:T(8,128)(2,1)S(1)} %get-tuple-element.23), channel_id=1, source_target_pairs={{0,24},{8,0},{16,8},{24,16},{1,25},{9,1},{17,9},{25,17},{2,26},{10... | collective-permute-start | bytes 393224 | tf_op jit(solution)/shard_map/ppermute | solution.py:377
  31.3 0.0 collective-permute-start.11
  31.3 1.0 %collective-permute-start.10 = (bf16[32,2048]{1,0:T(8,128)(2,1)S(1)}, bf16[32,2048]{1,0:T(8,128)(2,1)S(1)}, u32[]{:S(2)}, u32[]{:S(2)}) collective-permute-start(bf16[32,2048]{1,0:T(8,128)(2,1)S(1)} %get-tuple-element.25), channel_id=1, source_target_pairs={{0,16},{8,24},{16,0},{24,8},{1,17},{9,25},{17,1},{25,9},{2,18},{10... | collective-permute-start | bytes 393224 | tf_op jit(solution)/shard_map/ppermute | solution.py:377
  32.3 2.9 %collective-permute-done.9 = bf16[32,2048]{1,0:T(8,128)(2,1)S(1)} collective-permute-done((bf16[32,2048]{1,0:T(8,128)(2,1)S(1)}, bf16[32,2048]{1,0:T(8,128)(2,1)S(1)}, u32[]{:S(2)}, u32[]{:S(2)}) %collective-permute-start.9) | collective-permute-done | bytes 131104 | tf_op jit(solution)/shard_map/ppermute | solution.py:377
  35.2 4.3 %collective-permute-done.11 = bf16[32,2048]{1,0:T(8,128)(2,1)S(1)} collective-permute-done((bf16[32,2048]{1,0:T(8,128)(2,1)S(1)}, bf16[32,2048]{1,0:T(8,128)(2,1)S(1)}, u32[]{:S(2)}, u32[]{:S(2)}) %collective-permute-start.11) | collective-permute-done | bytes 131104 | tf_op jit(solution)/shard_map/ppermute | solution.py:377
  39.5 0.9 collective-permute-done.2
  40.4 0.1 add_convert_fusion.1
  40.5 2.1 %collective-permute-start.3 = (bf16[128,2048]{1,0:T(8,128)(2,1)S(1)}, bf16[128,2048]{1,0:T(8,128)(2,1)S(1)}, u32[]{:S(2)}, u32[]{:S(2)}) collective-permute-start(bf16[128,2048]{1,0:T(8,128)(2,1)S(1)} %add_convert_fusion.1), channel_id=1, source_target_pairs={{0,2},{1,5},{2,0},{3,7},{4,6},{5,1},{6,4},{7,3},{8,10},{9,13},{10,... | collective-permute-start | bytes 1572872 | tf_op jit(solution)/shard_map/ppermute | solution.py:374
  42.6 0.2 collective-permute-done.10
  42.8 0.9 collective-permute-start.19
  43.7 2.2 %collective-permute-start.14 = (bf16[128,1024]{1,0:T(8,128)(2,1)S(1)}, bf16[128,1024]{1,0:T(8,128)(2,1)S(1)}, u32[]{:S(2)}, u32[]{:S(2)}) collective-permute-start(bf16[128,1024]{1,0:T(8,128)(2,1)S(1)} %pad_maximum_fusion.refs_0_), channel_id=1, source_target_pairs={{0,6},{1,7},{2,4},{3,5},{4,2},{5,3},{6,0},{7,1},{8,14},{9,15},{10,... | collective-permute-start | bytes 786440 | tf_op jit(solution)/shard_map/ppermute | solution.py:374
  45.9 0.5 collective-permute-start.13
  46.4 0.8 collective-permute-start.12
  47.3 10.9 %collective-permute-done.19.refs_1_ = bf16[128,1024]{1,0:T(8,128)(2,1)S(1)} collective-permute-done((bf16[128,1024]{1,0:T(8,128)(2,1)S(1)}, bf16[128,1024]{1,0:T(8,128)(2,1)S(1)}, u32[]{:S(2)}, u32[]{:S(2)}) %collective-permute-start.19) | collective-permute-done | bytes 262176 | tf_op jit(solution)/shard_map/ppermute | solution.py:374
  58.2 2.0 %collective-permute-start.20 = (bf16[128,1024]{1,0:T(8,128)(2,1)S(1)}, bf16[128,1024]{1,0:T(8,128)(2,1)S(1)}, u32[]{:S(2)}, u32[]{:S(2)}) collective-permute-start(bf16[128,1024]{1,0:T(8,128)(2,1)S(1)} %pad_maximum_fusion.1.refs_0_), channel_id=1, source_target_pairs={{0,4},{1,3},{2,6},{3,1},{4,0},{5,7},{6,2},{7,5},{8,12},{9,11},{10,... | collective-permute-start | bytes 786440 | tf_op jit(solution)/shard_map/ppermute | solution.py:374
  60.2 0.0 collective-permute-start.21
  60.2 0.2 add_convert_fusion
  60.5 3.8 %collective-permute-done.14.refs_3_ = bf16[128,1024]{1,0:T(8,128)(2,1)S(1)} collective-permute-done((bf16[128,1024]{1,0:T(8,128)(2,1)S(1)}, bf16[128,1024]{1,0:T(8,128)(2,1)S(1)}, u32[]{:S(2)}, u32[]{:S(2)}) %collective-permute-start.14) | collective-permute-done | bytes 262176 | tf_op jit(solution)/shard_map/ppermute | solution.py:374
  64.2 0.0 collective-permute-start.22
  64.2 0.0 collective-permute-done.13.refs_2_
  64.2 0.5 collective-permute-start.24
  64.8 1.1 %collective-permute-done.20.refs_2_ = bf16[128,1024]{1,0:T(8,128)(2,1)S(1)} collective-permute-done((bf16[128,1024]{1,0:T(8,128)(2,1)S(1)}, bf16[128,1024]{1,0:T(8,128)(2,1)S(1)}, u32[]{:S(2)}, u32[]{:S(2)}) %collective-permute-start.20) | collective-permute-done | bytes 262176 | tf_op jit(solution)/shard_map/ppermute | solution.py:374
  65.8 2.8 %collective-permute-done.21.refs_3_ = bf16[128,1024]{1,0:T(8,128)(2,1)S(1)} collective-permute-done((bf16[128,1024]{1,0:T(8,128)(2,1)S(1)}, bf16[128,1024]{1,0:T(8,128)(2,1)S(1)}, u32[]{:S(2)}, u32[]{:S(2)}) %collective-permute-start.21) | collective-permute-done | bytes 262176 | tf_op jit(solution)/shard_map/ppermute | solution.py:374
  68.6 0.7 collective-permute-start.25
  69.3 4.3 %collective-permute-start.6 = (bf16[32,2048]{1,0:T(8,128)(2,1)S(1)}, bf16[32,2048]{1,0:T(8,128)(2,1)S(1)}, u32[]{:S(2)}, u32[]{:S(2)}) collective-permute-start(bf16[32,2048]{1,0:T(8,128)(2,1)S(1)} %get-tuple-element.27), channel_id=1, source_target_pairs={{0,24},{8,0},{16,8},{24,16},{1,25},{9,1},{17,9},{25,17},{2,26},{10... | collective-permute-start | bytes 393224 | tf_op jit(solution)/shard_map/ppermute | solution.py:377
  73.7 0.0 collective-permute-done.23.refs_5_
  73.7 0.1 collective-permute-start.15
  73.8 0.5 collective-permute-start.18
  74.3 0.1 collective-permute-start.16
  74.4 3.3 %collective-permute-done.6 = bf16[32,2048]{1,0:T(8,128)(2,1)S(1)} collective-permute-done((bf16[32,2048]{1,0:T(8,128)(2,1)S(1)}, bf16[32,2048]{1,0:T(8,128)(2,1)S(1)}, u32[]{:S(2)}, u32[]{:S(2)}) %collective-permute-start.6) | collective-permute-done | bytes 131104 | tf_op jit(solution)/shard_map/ppermute | solution.py:377
  77.6 4.7 %collective-permute-done.5 = bf16[32,2048]{1,0:T(8,128)(2,1)S(1)} collective-permute-done((bf16[32,2048]{1,0:T(8,128)(2,1)S(1)}, bf16[32,2048]{1,0:T(8,128)(2,1)S(1)}, u32[]{:S(2)}, u32[]{:S(2)}) %collective-permute-start.5) | collective-permute-done | bytes 131104 | tf_op jit(solution)/shard_map/ppermute | solution.py:377
  82.3 0.9 collective-permute-start.4
  83.2 7.3 %shard_map.94 = (f32[4096,1024]{1,0:T(8,128)}, f32[4096,1024]{1,0:T(8,128)}) custom-call(s32[1]{0:T(128)} %bitcast.place_ref, bf16[128,1024]{1,0:T(8,128)(2,1)S(1)} %pad_maximum_fusion.1.refs_0_, bf16[128,1024]{1,0:T(8,128)(2,1)S(1)} %collective-permute-done.19.refs_1_, bf16[128,1024]{1,0:T(8,128)(2,1)S(1)} %collective-permute-done.20.refs_2_, ...), custom_call_target="tpu_custom_call" | custom-call | flops 4294967296 | bytes 20971520 | tf_op jit(solution)/shard_map/pallas_call | solution.py:324
  90.6 0.2 convolution_convert_fusion.1
  90.8 0.1 collective-permute-start.7
  90.9 7.3 %shard_map.95 = (f32[4096,1024]{1,0:T(8,128)}, f32[4096,1024]{1,0:T(8,128)}) custom-call(s32[1]{0:T(128)} %bitcast.place_ref, bf16[128,1024]{1,0:T(8,128)(2,1)S(1)} %pad_maximum_fusion.refs_0_, bf16[128,1024]{1,0:T(8,128)(2,1)S(1)} %collective-permute-done.12.refs_1_, ...), custom_call_target="tpu_custom_call", output_to_operand_aliasing={{0}: (11, {}), {1}: (12, {})} | custom-call | flops 4294967296 | bytes 20971520 | tf_op jit(solution)/shard_map/pallas_call | solution.py:324
  98.3 0.7 pad_maximum_fusion.2
  (40 shorter events, 0.3 us)
Async XLA Ops:
  0.6 11.9 %copy-start.1 = (s32[24,2]{0,1:T(2,128)S(1)}, s32[24,2]{0,1:T(2,128)}, u32[]{:S(2)}) copy-start(s32[24,2]{0,1:T(2,128)} %param.8) | copy-start | bytes 580
  0.6 11.9 %copy-start = (bf16[24,4096]{1,0:T(8,128)(2,1)S(1)}, bf16[24,4096]{1,0:T(8,128)(2,1)}, u32[]{:S(2)}) copy-start(bf16[24,4096]{1,0:T(8,128)(2,1)} %param.7) | copy-start | bytes 589828
  0.7 11.9 %collective-permute-start = (s32[24,2]{0,1:T(2,128)}, s32[24,2]{0,1:T(2,128)S(1)}, u32[]{:S(2)}, u32[]{:S(2)}) collective-permute-start(s32[24,2]{0,1:T(2,128)} %param.8), channel_id=1, source_target_pairs={{0,1},{1,0},{2,3},{3,2},{4,5},{5,4},{6,7},{7,6},{8,9},{9,8},{10,11... | collective-permute-start | bytes 584 | tf_op jit(solution)/shard_map/ppermute | solution.py:368
  1.2 11.7 %collective-permute-start.8 = (bf16[24,4096]{1,0:T(8,128)(2,1)}, bf16[24,4096]{1,0:T(8,128)(2,1)S(1)}, u32[]{:S(2)}, u32[]{:S(2)}) collective-permute-start(bf16[24,4096]{1,0:T(8,128)(2,1)} %param.7), channel_id=1, source_target_pairs={{0,1},{1,0},{2,3},{3,2},{4,5},{5,4},{6,7},{7,6},{8,9},{9,8},{10,11... | collective-permute-start | bytes 589832 | tf_op jit(solution)/shard_map/ppermute | solution.py:368
  11.9 4.6 %collective-permute-start.1 = (bf16[512,2048]{1,0:T(8,128)(2,1)}, bf16[512,2048]{1,0:T(8,128)(2,1)}, u32[]{:S(2)}, u32[]{:S(2)}) collective-permute-start(bf16[512,2048]{1,0:T(8,128)(2,1)} %get-tuple-element.14), channel_id=1, source_target_pairs={{0,1},{1,0},{2,3},{3,2},{4,5},{5,4},{6,7},{7,6},{8,9},{9,8},{10,11... | collective-permute-start | bytes 6291464 | tf_op jit(solution)/shard_map/ppermute | solution.py:368
  24.7 15.7 %collective-permute-start.2 = (bf16[256,2048]{1,0:T(8,128)(2,1)S(1)}, bf16[256,2048]{1,0:T(8,128)(2,1)S(1)}, u32[]{:S(2)}, u32[]{:S(2)}) collective-permute-start(bf16[256,2048]{1,0:T(8,128)(2,1)S(1)} %get-tuple-element.16), channel_id=1, source_target_pairs={{0,4},{1,3},{2,6},{3,1},{4,0},{5,7},{6,2},{7,5},{8,12},{9,11},{10,... | collective-permute-start | bytes 3145736 | tf_op jit(solution)/shard_map/ppermute | solution.py:374
  27.6 7.5 %collective-permute-start.9 = (bf16[32,2048]{1,0:T(8,128)(2,1)S(1)}, bf16[32,2048]{1,0:T(8,128)(2,1)S(1)}, u32[]{:S(2)}, u32[]{:S(2)}) collective-permute-start(bf16[32,2048]{1,0:T(8,128)(2,1)S(1)} %get-tuple-element.23), channel_id=1, source_target_pairs={{0,24},{8,0},{16,8},{24,16},{1,25},{9,1},{17,9},{25,17},{2,26},{10... | collective-permute-start | bytes 393224 | tf_op jit(solution)/shard_map/ppermute | solution.py:377
  31.3 8.2 %collective-permute-start.11 = (bf16[32,2048]{1,0:T(8,128)(2,1)S(1)}, bf16[32,2048]{1,0:T(8,128)(2,1)S(1)}, u32[]{:S(2)}, u32[]{:S(2)}) collective-permute-start(bf16[32,2048]{1,0:T(8,128)(2,1)S(1)} %get-tuple-element.24), channel_id=1, source_target_pairs={{0,8},{8,16},{16,24},{24,0},{1,9},{9,17},{17,25},{25,1},{2,10},{10... | collective-permute-start | bytes 393224 | tf_op jit(solution)/shard_map/ppermute | solution.py:377
  31.3 11.5 %collective-permute-start.10 = (bf16[32,2048]{1,0:T(8,128)(2,1)S(1)}, bf16[32,2048]{1,0:T(8,128)(2,1)S(1)}, u32[]{:S(2)}, u32[]{:S(2)}) collective-permute-start(bf16[32,2048]{1,0:T(8,128)(2,1)S(1)} %get-tuple-element.25), channel_id=1, source_target_pairs={{0,16},{8,24},{16,0},{24,8},{1,17},{9,25},{17,1},{25,9},{2,18},{10... | collective-permute-start | bytes 393224 | tf_op jit(solution)/shard_map/ppermute | solution.py:377
  40.5 19.7 %collective-permute-start.3 = (bf16[128,2048]{1,0:T(8,128)(2,1)S(1)}, bf16[128,2048]{1,0:T(8,128)(2,1)S(1)}, u32[]{:S(2)}, u32[]{:S(2)}) collective-permute-start(bf16[128,2048]{1,0:T(8,128)(2,1)S(1)} %add_convert_fusion.1), channel_id=1, source_target_pairs={{0,2},{1,5},{2,0},{3,7},{4,6},{5,1},{6,4},{7,3},{8,10},{9,13},{10,... | collective-permute-start | bytes 1572872 | tf_op jit(solution)/shard_map/ppermute | solution.py:374
  42.8 15.4 %collective-permute-start.19 = (bf16[128,1024]{1,0:T(8,128)(2,1)S(1)}, bf16[128,1024]{1,0:T(8,128)(2,1)S(1)}, u32[]{:S(2)}, u32[]{:S(2)}) collective-permute-start(bf16[128,1024]{1,0:T(8,128)(2,1)S(1)} %pad_maximum_fusion.1.refs_0_), channel_id=1, source_target_pairs={{0,2},{1,5},{2,0},{3,7},{4,6},{5,1},{6,4},{7,3},{8,10},{9,13},{10,... | collective-permute-start | bytes 786440 | tf_op jit(solution)/shard_map/ppermute | solution.py:374
  43.7 20.5 %collective-permute-start.14 = (bf16[128,1024]{1,0:T(8,128)(2,1)S(1)}, bf16[128,1024]{1,0:T(8,128)(2,1)S(1)}, u32[]{:S(2)}, u32[]{:S(2)}) collective-permute-start(bf16[128,1024]{1,0:T(8,128)(2,1)S(1)} %pad_maximum_fusion.refs_0_), channel_id=1, source_target_pairs={{0,6},{1,7},{2,4},{3,5},{4,2},{5,3},{6,0},{7,1},{8,14},{9,15},{10,... | collective-permute-start | bytes 786440 | tf_op jit(solution)/shard_map/ppermute | solution.py:374
  45.9 18.3 %collective-permute-start.13 = (bf16[128,1024]{1,0:T(8,128)(2,1)S(1)}, bf16[128,1024]{1,0:T(8,128)(2,1)S(1)}, u32[]{:S(2)}, u32[]{:S(2)}) collective-permute-start(bf16[128,1024]{1,0:T(8,128)(2,1)S(1)} %pad_maximum_fusion.refs_0_), channel_id=1, source_target_pairs={{0,4},{1,3},{2,6},{3,1},{4,0},{5,7},{6,2},{7,5},{8,12},{9,11},{10,... | collective-permute-start | bytes 786440 | tf_op jit(solution)/shard_map/ppermute | solution.py:374
  46.4 22.9 %collective-permute-start.12 = (bf16[128,1024]{1,0:T(8,128)(2,1)S(1)}, bf16[128,1024]{1,0:T(8,128)(2,1)S(1)}, u32[]{:S(2)}, u32[]{:S(2)}) collective-permute-start(bf16[128,1024]{1,0:T(8,128)(2,1)S(1)} %pad_maximum_fusion.refs_0_), channel_id=1, source_target_pairs={{0,2},{1,5},{2,0},{3,7},{4,6},{5,1},{6,4},{7,3},{8,10},{9,13},{10,... | collective-permute-start | bytes 786440 | tf_op jit(solution)/shard_map/ppermute | solution.py:374
  58.2 7.6 %collective-permute-start.20 = (bf16[128,1024]{1,0:T(8,128)(2,1)S(1)}, bf16[128,1024]{1,0:T(8,128)(2,1)S(1)}, u32[]{:S(2)}, u32[]{:S(2)}) collective-permute-start(bf16[128,1024]{1,0:T(8,128)(2,1)S(1)} %pad_maximum_fusion.1.refs_0_), channel_id=1, source_target_pairs={{0,4},{1,3},{2,6},{3,1},{4,0},{5,7},{6,2},{7,5},{8,12},{9,11},{10,... | collective-permute-start | bytes 786440 | tf_op jit(solution)/shard_map/ppermute | solution.py:374
  60.2 8.4 %collective-permute-start.21 = (bf16[128,1024]{1,0:T(8,128)(2,1)S(1)}, bf16[128,1024]{1,0:T(8,128)(2,1)S(1)}, u32[]{:S(2)}, u32[]{:S(2)}) collective-permute-start(bf16[128,1024]{1,0:T(8,128)(2,1)S(1)} %collective-permute-done.19.refs_1_), channel_id=1, source_target_pairs={{0,4},{1,3},{2,6},{3,1},{4,0},{5,7},{6,2},{7,5},{8,12},{9,11},{10,... | collective-permute-start | bytes 786440 | tf_op jit(solution)/shard_map/ppermute | solution.py:374
  64.2 9.5 %collective-permute-start.22 = (bf16[128,1024]{1,0:T(8,128)(2,1)S(1)}, bf16[128,1024]{1,0:T(8,128)(2,1)S(1)}, u32[]{:S(2)}, u32[]{:S(2)}) collective-permute-start(bf16[128,1024]{1,0:T(8,128)(2,1)S(1)} %pad_maximum_fusion.1.refs_0_), channel_id=1, source_target_pairs={{0,1},{1,0},{2,3},{3,2},{4,5},{5,4},{6,7},{7,6},{8,9},{9,8},{10,11... | collective-permute-start | bytes 786440 | tf_op jit(solution)/shard_map/ppermute | solution.py:368
  64.2 9.5 %collective-permute-start.24 = (bf16[128,1024]{1,0:T(8,128)(2,1)S(1)}, bf16[128,1024]{1,0:T(8,128)(2,1)S(1)}, u32[]{:S(2)}, u32[]{:S(2)}) collective-permute-start(bf16[128,1024]{1,0:T(8,128)(2,1)S(1)} %collective-permute-done.19.refs_1_), channel_id=1, source_target_pairs={{0,1},{1,0},{2,3},{3,2},{4,5},{5,4},{6,7},{7,6},{8,9},{9,8},{10,11... | collective-permute-start | bytes 786440 | tf_op jit(solution)/shard_map/ppermute | solution.py:368
  65.8 7.9 %collective-permute-start.23 = (bf16[128,1024]{1,0:T(8,128)(2,1)S(1)}, bf16[128,1024]{1,0:T(8,128)(2,1)S(1)}, u32[]{:S(2)}, u32[]{:S(2)}) collective-permute-start(bf16[128,1024]{1,0:T(8,128)(2,1)S(1)} %collective-permute-done.20.refs_2_), channel_id=1, source_target_pairs={{0,1},{1,0},{2,3},{3,2},{4,5},{5,4},{6,7},{7,6},{8,9},{9,8},{10,11... | collective-permute-start | bytes 786440 | tf_op jit(solution)/shard_map/ppermute | solution.py:368
  68.6 5.7 %collective-permute-start.25 = (bf16[128,1024]{1,0:T(8,128)(2,1)S(1)}, bf16[128,1024]{1,0:T(8,128)(2,1)S(1)}, u32[]{:S(2)}, u32[]{:S(2)}) collective-permute-start(bf16[128,1024]{1,0:T(8,128)(2,1)S(1)} %collective-permute-done.21.refs_3_), channel_id=1, source_target_pairs={{0,1},{1,0},{2,3},{3,2},{4,5},{5,4},{6,7},{7,6},{8,9},{9,8},{10,11... | collective-permute-start | bytes 786440 | tf_op jit(solution)/shard_map/ppermute | solution.py:368
  69.3 8.3 %collective-permute-start.6 = (bf16[32,2048]{1,0:T(8,128)(2,1)S(1)}, bf16[32,2048]{1,0:T(8,128)(2,1)S(1)}, u32[]{:S(2)}, u32[]{:S(2)}) collective-permute-start(bf16[32,2048]{1,0:T(8,128)(2,1)S(1)} %get-tuple-element.27), channel_id=1, source_target_pairs={{0,24},{8,0},{16,8},{24,16},{1,25},{9,1},{17,9},{25,17},{2,26},{10... | collective-permute-start | bytes 393224 | tf_op jit(solution)/shard_map/ppermute | solution.py:377
  73.7 8.6 %collective-permute-start.5 = (bf16[32,2048]{1,0:T(8,128)(2,1)S(1)}, bf16[32,2048]{1,0:T(8,128)(2,1)S(1)}, u32[]{:S(2)}, u32[]{:S(2)}) collective-permute-start(bf16[32,2048]{1,0:T(8,128)(2,1)S(1)} %get-tuple-element.28), channel_id=1, source_target_pairs={{0,16},{8,24},{16,0},{24,8},{1,17},{9,25},{17,1},{25,9},{2,18},{10... | collective-permute-start | bytes 393224 | tf_op jit(solution)/shard_map/ppermute | solution.py:377
  73.7 17.2 %collective-permute-start.15 = (bf16[128,1024]{1,0:T(8,128)(2,1)S(1)}, bf16[128,1024]{1,0:T(8,128)(2,1)S(1)}, u32[]{:S(2)}, u32[]{:S(2)}) collective-permute-start(bf16[128,1024]{1,0:T(8,128)(2,1)S(1)} %pad_maximum_fusion.refs_0_), channel_id=1, source_target_pairs={{0,1},{1,0},{2,3},{3,2},{4,5},{5,4},{6,7},{7,6},{8,9},{9,8},{10,11... | collective-permute-start | bytes 786440 | tf_op jit(solution)/shard_map/ppermute | solution.py:368
  73.8 17.1 %collective-permute-start.18 = (bf16[128,1024]{1,0:T(8,128)(2,1)S(1)}, bf16[128,1024]{1,0:T(8,128)(2,1)S(1)}, u32[]{:S(2)}, u32[]{:S(2)}) collective-permute-start(bf16[128,1024]{1,0:T(8,128)(2,1)S(1)} %collective-permute-done.14.refs_3_), channel_id=1, source_target_pairs={{0,1},{1,0},{2,3},{3,2},{4,5},{5,4},{6,7},{7,6},{8,9},{9,8},{10,11... | collective-permute-start | bytes 786440 | tf_op jit(solution)/shard_map/ppermute | solution.py:368
  74.3 16.6 %collective-permute-start.16 = (bf16[128,1024]{1,0:T(8,128)(2,1)S(1)}, bf16[128,1024]{1,0:T(8,128)(2,1)S(1)}, u32[]{:S(2)}, u32[]{:S(2)}) collective-permute-start(bf16[128,1024]{1,0:T(8,128)(2,1)S(1)} %collective-permute-done.13.refs_2_), channel_id=1, source_target_pairs={{0,1},{1,0},{2,3},{3,2},{4,5},{5,4},{6,7},{7,6},{8,9},{9,8},{10,11... | collective-permute-start | bytes 786440 | tf_op jit(solution)/shard_map/ppermute | solution.py:368
  77.6 13.3 %collective-permute-start.17 = (bf16[128,1024]{1,0:T(8,128)(2,1)S(1)}, bf16[128,1024]{1,0:T(8,128)(2,1)S(1)}, u32[]{:S(2)}, u32[]{:S(2)}) collective-permute-start(bf16[128,1024]{1,0:T(8,128)(2,1)S(1)} %collective-permute-done.12.refs_1_), channel_id=1, source_target_pairs={{0,1},{1,0},{2,3},{3,2},{4,5},{5,4},{6,7},{7,6},{8,9},{9,8},{10,11... | collective-permute-start | bytes 786440 | tf_op jit(solution)/shard_map/ppermute | solution.py:368
  82.3 8.2 %collective-permute-start.4 = (bf16[32,2048]{1,0:T(8,128)(2,1)S(1)}, bf16[32,2048]{1,0:T(8,128)(2,1)S(1)}, u32[]{:S(2)}, u32[]{:S(2)}) collective-permute-start(bf16[32,2048]{1,0:T(8,128)(2,1)S(1)} %get-tuple-element.29), channel_id=1, source_target_pairs={{0,8},{8,16},{16,24},{24,0},{1,9},{9,17},{17,25},{25,1},{2,10},{10... | collective-permute-start | bytes 393224 | tf_op jit(solution)/shard_map/ppermute | solution.py:377
  90.8 7.5 %collective-permute-start.7 = (bf16[24,2048]{1,0:T(8,128)(2,1)S(1)}, bf16[24,2048]{1,0:T(8,128)(2,1)S(1)}, u32[]{:S(2)}, u32[]{:S(2)}) collective-permute-start(bf16[24,2048]{1,0:T(8,128)(2,1)S(1)} %slice.110), channel_id=1, source_target_pairs={{0,1},{1,0},{2,3},{3,2},{4,5},{5,4},{6,7},{7,6},{8,9},{9,8},{10,11... | collective-permute-start | bytes 294920 | tf_op jit(solution)/shard_map/ppermute | solution.py:368

commit v3 on v2

--- a/solution.py
+++ b/solution.py
@@ -14,7 +14,7 @@
     return pltpu.CompilerParams(vmem_limit_bytes=mebibytes * 1024 * 1024)
 
 
-DIRECT = (False, True)
+DIRECT = (False, False)
 
 
 def block_width(width, limit):
@@ -91,9 +91,11 @@
     return copies
 
 
-def block_product(grads_ref, weights_ref, loads, step, block):
+def block_product(grads_ref, weights_ref, loads, step, block, ready=()):
     acc = None
     for n in range(2):
+        for copy in ready[n : n + 1]:
+            copy.wait()
         loads[2 * step + n].wait()
         for copy in loads[2 * step + n + 2 : 2 * step + n + 3]:
             copy.start()
@@ -136,7 +138,7 @@
         for v in range(chips):
             for copy in loads[3 * v : 3 * v + 3]:
                 copy.wait()
-            if v == chips - 1:
+            if v == 0:
                 for copy in weights[:2]:
                     copy.start()
             swiglu_rows(place_ref, shards, v, source_ref, grads_ref, groups, capacity)
@@ -214,12 +216,11 @@
         ]
         for copy in [grads[0], weights[0], grads[1], weights[1], *added[:2]]:
             copy.start()
-        for copy in grads:
-            copy.wait()
         outs = []
         for step in range(steps):
             slot = step % 2
-            acc = block_product(grads_ref, weights_ref, weights, step, block)
+            ready = grads if step == 0 else ()
+            acc = block_product(grads_ref, weights_ref, weights, step, block, ready)
             added[step].wait()
             if step >= 2:
                 for copy in outs[step - 2]:
@@ -428,7 +429,7 @@
         columns = slice(part * part_width, (part + 1) * part_width)
         held = {0: jnp.concatenate([rows[:, columns] for rows in arrived], axis=0)}
         for v in masks[1:]:
-            bit = v if DIRECT[part] else 1 << v.bit_length() - 1
+            bit = v if DIRECT[part] else v & -v
             held[v] = over_plane(held[v ^ bit], bit)
         swapped = {}
         for v in masks:

time: 99.2 us -> 93.4 us (0.942)
  waiting for transfers between devices: 38 us -> 31.9 us
  starting transfers between devices: 24.4 us -> 25.5 us
    ppermute x8, waiting for transfers between devices: 19.4 us -> 14.1 us  [over_plane(): lax.ppermute(value, 'shard', [(i, i ^ masks[i & 1]) for i in range(shards)])]
    ppermute x6, starting transfers between devices: 9.91 us -> 11.2 us  [over_expert(): lax.ppermute(value, 'expert', [(i, (i + step) % groups) for i in range(gr...]
    ppermute x12, starting transfers between devices: 3.04 us -> 1.79 us  [over_core(): return lax.ppermute(value, 'shard', [(i, i ^ 1) for i in range(shards)])]
    ppermute x8, starting transfers between devices: 11.5 us -> 12.5 us  [over_plane(): lax.ppermute(value, 'shard', [(i, i ^ masks[i & 1]) for i in range(shards)])]
  transfers between devices with their start and end apart: 26 -> 26, of which waited for: 11 -> 13; matrix products, arithmetic and copies ran while one was open for 2% -> 2% of each run, Pallas kernels for 26% -> 26%
where the time goes in v3:
time: 93.4 us; the launch traced here: 93.1 us
  Pallas kernels  32.5 us (35%)
  waiting for transfers between devices  31.9 us (34%)
  starting transfers between devices  25.5 us (27%)
  other arithmetic  1.33 us (1%)
  between operations  0.94 us (1%)
    pallas_call x2, Pallas kernels, wgrad(): pl.pallas_call(kernel, in_specs=[pl.BlockSpec(memory_space=pltpu.SMEM)] +...  14.6 us
    ppermute x6, waiting for transfers between devices, over_expert(): lax.ppermute(value, 'expert', [(i, (i + step) % groups) for i in range(gr...  14.6 us
    ppermute x8, waiting for transfers between devices, over_plane(): lax.ppermute(value, 'shard', [(i, i ^ masks[i & 1]) for i in range(shards)])  14.1 us
    ppermute x8, starting transfers between devices, over_plane(): lax.ppermute(value, 'shard', [(i, i ^ masks[i & 1]) for i in range(shards)])  12.5 us
    ppermute x6, starting transfers between devices, over_expert(): lax.ppermute(value, 'expert', [(i, (i + step) % groups) for i in range(gr...  11.2 us
    pallas_call x1, Pallas kernels, dgrad_other(): pl.pallas_call(kernel, name='dgrad_other', in_specs=[pl.BlockSpec(memory_...  9.76 us
    pallas_call x1, Pallas kernels, dgrad_own(): pl.pallas_call(kernel, name='dgrad_own', in_specs=[pl.BlockSpec(memory_sp...  8.11 us
    ppermute x12, waiting for transfers between devices, over_core(): return lax.ppermute(value, 'shard', [(i, i ^ 1) for i in range(shards)])  3.27 us
  transfers between devices with their start and end apart: 26, of which 13 were waited for; matrix products, arithmetic and copies ran while one was open for 2% of the time, Pallas kernels for 26%

profile of v3, /device:TPU:0, one launch (start us, length us, event | category | flops | bytes accessed | tf_op | source)
XLA Modules:
  0.0 93.1 jit_solution(18018330369772199306)
XLA Ops:
  0.7 0.6 collective-permute-start
  1.2 0.1 collective-permute-start.8
  1.3 9.8 %dgrad_other.1 = (bf16[512,1024]{1,0:T(8,128)(2,1)S(1)}, bf16[512,1024]{1,0:T(8,128)(2,1)S(1)}, bf16[512,2048]{1,0:T(8,128)(2,1)}) custom-call(s32[1]{0:T(128)} %bitcast.place_ref, bf16[512,1024]{1,0:T(8,128)(2,1)} %bitcast.16, bf16[512,1024]{1,0:T(8,128)(2,1)} %bitcast.17, bf16[512,1024]{1,0:T(8,128)(2,1)} %bitcast.18, bf16[4096,1024]{1,0:T(8,128)(2,1)} %bitcast.10, ...), custom_call_target="tpu_custom_call" | custom-call | flops 4294967296 | bytes 15728640 | tf_op jit(solution)/shard_map/dgrad_other/pallas_call | solution.py:173
  11.1 0.5 collective-permute-start.1
  11.7 0.0 collective-permute-done
  11.7 0.1 compare_select_fusion
  11.8 0.1 compare_reduce_fusion
  11.9 0.2 fusion
  12.1 0.0 collective-permute-done.8
  12.1 0.3 convolution_convert_fusion
  12.4 3.2 %collective-permute-done.1.came_ref = bf16[512,2048]{1,0:T(8,128)(2,1)} collective-permute-done((bf16[512,2048]{1,0:T(8,128)(2,1)}, bf16[512,2048]{1,0:T(8,128)(2,1)}, u32[]{:S(2)}, u32[]{:S(2)}) %collective-permute-start.1) | collective-permute-done | bytes 2097184 | tf_op jit(solution)/shard_map/ppermute | solution.py:369
  15.7 8.1 %dgrad_own.1 = (bf16[256,2048]{1,0:T(8,128)(2,1)S(1)}, bf16[256,2048]{1,0:T(8,128)(2,1)S(1)}) custom-call(s32[1]{0:T(128)} %bitcast.place_ref, bf16[512,1024]{1,0:T(8,128)(2,1)S(1)} %get-tuple-element.12.gate_ref.refs_8_, bf16[512,1024]{1,0:T(8,128)(2,1)S(1)} %get-tuple-element.13.up_ref.refs_9_, bf16[4096,1024]{1,0:T(8,128)(2,1)} %bitcast.11, ...), custom_call_target="tpu_custom_call" | custom-call | flops 4294967296 | bytes 14680064 | tf_op jit(solution)/shard_map/dgrad_own/pallas_call | solution.py:247
  23.8 2.9 %collective-permute-start.2 = (bf16[256,2048]{1,0:T(8,128)(2,1)S(1)}, bf16[256,2048]{1,0:T(8,128)(2,1)S(1)}, u32[]{:S(2)}, u32[]{:S(2)}) collective-permute-start(bf16[256,2048]{1,0:T(8,128)(2,1)S(1)} %get-tuple-element.16), channel_id=1, source_target_pairs={{0,4},{1,3},{2,6},{3,1},{4,0},{5,7},{6,2},{7,5},{8,12},{9,11},{10,... | collective-permute-start | bytes 3145736 | tf_op jit(solution)/shard_map/ppermute | solution.py:375
  26.8 3.6 %collective-permute-start.9 = (bf16[32,2048]{1,0:T(8,128)(2,1)S(1)}, bf16[32,2048]{1,0:T(8,128)(2,1)S(1)}, u32[]{:S(2)}, u32[]{:S(2)}) collective-permute-start(bf16[32,2048]{1,0:T(8,128)(2,1)S(1)} %get-tuple-element.23), channel_id=1, source_target_pairs={{0,24},{8,0},{16,8},{24,16},{1,25},{9,1},{17,9},{25,17},{2,26},{10... | collective-permute-start | bytes 393224 | tf_op jit(solution)/shard_map/ppermute | solution.py:378
  30.4 0.0 collective-permute-start.11
  30.4 1.0 %collective-permute-start.10 = (bf16[32,2048]{1,0:T(8,128)(2,1)S(1)}, bf16[32,2048]{1,0:T(8,128)(2,1)S(1)}, u32[]{:S(2)}, u32[]{:S(2)}) collective-permute-start(bf16[32,2048]{1,0:T(8,128)(2,1)S(1)} %get-tuple-element.25), channel_id=1, source_target_pairs={{0,16},{8,24},{16,0},{24,8},{1,17},{9,25},{17,1},{25,9},{2,18},{10... | collective-permute-start | bytes 393224 | tf_op jit(solution)/shard_map/ppermute | solution.py:378
  31.5 2.9 %collective-permute-done.9 = bf16[32,2048]{1,0:T(8,128)(2,1)S(1)} collective-permute-done((bf16[32,2048]{1,0:T(8,128)(2,1)S(1)}, bf16[32,2048]{1,0:T(8,128)(2,1)S(1)}, u32[]{:S(2)}, u32[]{:S(2)}) %collective-permute-start.9) | collective-permute-done | bytes 131104 | tf_op jit(solution)/shard_map/ppermute | solution.py:378
  34.3 4.3 %collective-permute-done.11 = bf16[32,2048]{1,0:T(8,128)(2,1)S(1)} collective-permute-done((bf16[32,2048]{1,0:T(8,128)(2,1)S(1)}, bf16[32,2048]{1,0:T(8,128)(2,1)S(1)}, u32[]{:S(2)}, u32[]{:S(2)}) %collective-permute-start.11) | collective-permute-done | bytes 131104 | tf_op jit(solution)/shard_map/ppermute | solution.py:378
  38.7 0.9 collective-permute-done.2
  39.5 0.1 add_convert_fusion.1
  39.7 2.0 %collective-permute-start.3 = (bf16[128,2048]{1,0:T(8,128)(2,1)S(1)}, bf16[128,2048]{1,0:T(8,128)(2,1)S(1)}, u32[]{:S(2)}, u32[]{:S(2)}) collective-permute-start(bf16[128,2048]{1,0:T(8,128)(2,1)S(1)} %add_convert_fusion.1), channel_id=1, source_target_pairs={{0,2},{1,5},{2,0},{3,7},{4,6},{5,1},{6,4},{7,3},{8,10},{9,13},{10,... | collective-permute-start | bytes 1572872 | tf_op jit(solution)/shard_map/ppermute | solution.py:375
  41.7 0.2 collective-permute-done.10
  41.9 1.6 %collective-permute-start.20 = (bf16[128,1024]{1,0:T(8,128)(2,1)S(1)}, bf16[128,1024]{1,0:T(8,128)(2,1)S(1)}, u32[]{:S(2)}, u32[]{:S(2)}) collective-permute-start(bf16[128,1024]{1,0:T(8,128)(2,1)S(1)} %pad_maximum_fusion.1.refs_0_), channel_id=1, source_target_pairs={{0,4},{1,3},{2,6},{3,1},{4,0},{5,7},{6,2},{7,5},{8,12},{9,11},{10,... | collective-permute-start | bytes 786440 | tf_op jit(solution)/shard_map/ppermute | solution.py:375
  43.5 0.6 collective-permute-start.13
  44.1 0.8 collective-permute-start.12
  44.9 0.0 collective-permute-start.22
  44.9 6.2 %collective-permute-done.20.refs_2_ = bf16[128,1024]{1,0:T(8,128)(2,1)S(1)} collective-permute-done((bf16[128,1024]{1,0:T(8,128)(2,1)S(1)}, bf16[128,1024]{1,0:T(8,128)(2,1)S(1)}, u32[]{:S(2)}, u32[]{:S(2)}) %collective-permute-start.20) | collective-permute-done | bytes 262176 | tf_op jit(solution)/shard_map/ppermute | solution.py:375
  51.2 0.8 collective-permute-start.19
  52.0 2.1 %collective-permute-done.3 = bf16[128,2048]{1,0:T(8,128)(2,1)S(1)} collective-permute-done((bf16[128,2048]{1,0:T(8,128)(2,1)S(1)}, bf16[128,2048]{1,0:T(8,128)(2,1)S(1)}, u32[]{:S(2)}, u32[]{:S(2)}) %collective-permute-start.3) | collective-permute-done | bytes 524320 | tf_op jit(solution)/shard_map/ppermute | solution.py:375
  54.1 2.1 %collective-permute-start.21 = (bf16[128,1024]{1,0:T(8,128)(2,1)S(1)}, bf16[128,1024]{1,0:T(8,128)(2,1)S(1)}, u32[]{:S(2)}, u32[]{:S(2)}) collective-permute-start(bf16[128,1024]{1,0:T(8,128)(2,1)S(1)} %collective-permute-done.20.refs_2_), channel_id=1, source_target_pairs={{0,2},{1,5},{2,0},{3,7},{4,6},{5,1},{6,4},{7,3},{8,10},{9,13},{10,... | collective-permute-start | bytes 786440 | tf_op jit(solution)/shard_map/ppermute | solution.py:375
  56.2 0.2 add_convert_fusion
  56.4 0.4 collective-permute-done.13.refs_2_
  56.8 0.5 collective-permute-done.12.refs_1_
  57.3 1.7 %collective-permute-start.14 = (bf16[128,1024]{1,0:T(8,128)(2,1)S(1)}, bf16[128,1024]{1,0:T(8,128)(2,1)S(1)}, u32[]{:S(2)}, u32[]{:S(2)}) collective-permute-start(bf16[128,1024]{1,0:T(8,128)(2,1)S(1)} %collective-permute-done.13.refs_2_), channel_id=1, source_target_pairs={{0,2},{1,5},{2,0},{3,7},{4,6},{5,1},{6,4},{7,3},{8,10},{9,13},{10,... | collective-permute-start | bytes 786440 | tf_op jit(solution)/shard_map/ppermute | solution.py:375
  59.0 1.2 %collective-permute-done.19.refs_1_ = bf16[128,1024]{1,0:T(8,128)(2,1)S(1)} collective-permute-done((bf16[128,1024]{1,0:T(8,128)(2,1)S(1)}, bf16[128,1024]{1,0:T(8,128)(2,1)S(1)}, u32[]{:S(2)}, u32[]{:S(2)}) %collective-permute-start.19) | collective-permute-done | bytes 262176 | tf_op jit(solution)/shard_map/ppermute | solution.py:375
  60.1 2.8 %collective-permute-done.21.refs_3_ = bf16[128,1024]{1,0:T(8,128)(2,1)S(1)} collective-permute-done((bf16[128,1024]{1,0:T(8,128)(2,1)S(1)}, bf16[128,1024]{1,0:T(8,128)(2,1)S(1)}, u32[]{:S(2)}, u32[]{:S(2)}) %collective-permute-start.21) | collective-permute-done | bytes 262176 | tf_op jit(solution)/shard_map/ppermute | solution.py:375
  63.0 4.0 %collective-permute-start.6 = (bf16[32,2048]{1,0:T(8,128)(2,1)S(1)}, bf16[32,2048]{1,0:T(8,128)(2,1)S(1)}, u32[]{:S(2)}, u32[]{:S(2)}) collective-permute-start(bf16[32,2048]{1,0:T(8,128)(2,1)S(1)} %get-tuple-element.27), channel_id=1, source_target_pairs={{0,24},{8,0},{16,8},{24,16},{1,25},{9,1},{17,9},{25,17},{2,26},{10... | collective-permute-start | bytes 393224 | tf_op jit(solution)/shard_map/ppermute | solution.py:378
  67.0 1.5 %collective-permute-start.5 = (bf16[32,2048]{1,0:T(8,128)(2,1)S(1)}, bf16[32,2048]{1,0:T(8,128)(2,1)S(1)}, u32[]{:S(2)}, u32[]{:S(2)}) collective-permute-start(bf16[32,2048]{1,0:T(8,128)(2,1)S(1)} %get-tuple-element.28), channel_id=1, source_target_pairs={{0,16},{8,24},{16,0},{24,8},{1,17},{9,25},{17,1},{25,9},{2,18},{10... | collective-permute-start | bytes 393224 | tf_op jit(solution)/shard_map/ppermute | solution.py:378
  68.5 0.5 collective-permute-start.16
  69.0 0.1 collective-permute-start.17
  69.1 1.8 %collective-permute-done.6 = bf16[32,2048]{1,0:T(8,128)(2,1)S(1)} collective-permute-done((bf16[32,2048]{1,0:T(8,128)(2,1)S(1)}, bf16[32,2048]{1,0:T(8,128)(2,1)S(1)}, u32[]{:S(2)}, u32[]{:S(2)}) %collective-permute-start.6) | collective-permute-done | bytes 131104 | tf_op jit(solution)/shard_map/ppermute | solution.py:378
  70.9 5.4 %collective-permute-done.5 = bf16[32,2048]{1,0:T(8,128)(2,1)S(1)} collective-permute-done((bf16[32,2048]{1,0:T(8,128)(2,1)S(1)}, bf16[32,2048]{1,0:T(8,128)(2,1)S(1)}, u32[]{:S(2)}, u32[]{:S(2)}) %collective-permute-start.5) | collective-permute-done | bytes 131104 | tf_op jit(solution)/shard_map/ppermute | solution.py:378
  76.3 1.0 %collective-permute-start.4 = (bf16[32,2048]{1,0:T(8,128)(2,1)S(1)}, bf16[32,2048]{1,0:T(8,128)(2,1)S(1)}, u32[]{:S(2)}, u32[]{:S(2)}) collective-permute-start(bf16[32,2048]{1,0:T(8,128)(2,1)S(1)} %get-tuple-element.29), channel_id=1, source_target_pairs={{0,8},{8,16},{16,24},{24,0},{1,9},{9,17},{17,25},{25,1},{2,10},{10... | collective-permute-start | bytes 393224 | tf_op jit(solution)/shard_map/ppermute | solution.py:378
  77.4 7.3 %shard_map.94 = (f32[4096,1024]{1,0:T(8,128)}, f32[4096,1024]{1,0:T(8,128)}) custom-call(s32[1]{0:T(128)} %bitcast.place_ref, bf16[128,1024]{1,0:T(8,128)(2,1)S(1)} %pad_maximum_fusion.1.refs_0_, bf16[128,1024]{1,0:T(8,128)(2,1)S(1)} %collective-permute-done.19.refs_1_, bf16[128,1024]{1,0:T(8,128)(2,1)S(1)} %collective-permute-done.20.refs_2_, ...), custom_call_target="tpu_custom_call" | custom-call | flops 4294967296 | bytes 20971520 | tf_op jit(solution)/shard_map/pallas_call | solution.py:325
  84.7 0.2 convolution_convert_fusion.1
  84.9 0.1 collective-permute-start.7
  85.1 7.3 %shard_map.95 = (f32[4096,1024]{1,0:T(8,128)}, f32[4096,1024]{1,0:T(8,128)}) custom-call(s32[1]{0:T(128)} %bitcast.place_ref, bf16[128,1024]{1,0:T(8,128)(2,1)S(1)} %pad_maximum_fusion.refs_0_, bf16[128,1024]{1,0:T(8,128)(2,1)S(1)} %collective-permute-done.12.refs_1_, ...), custom_call_target="tpu_custom_call", output_to_operand_aliasing={{0}: (11, {}), {1}: (12, {})} | custom-call | flops 4294967296 | bytes 20971520 | tf_op jit(solution)/shard_map/pallas_call | solution.py:325
  92.4 0.7 pad_maximum_fusion.2
  (40 shorter events, 0.3 us)
Async XLA Ops:
  0.6 11.1 %copy-start.1 = (s32[24,2]{0,1:T(2,128)S(1)}, s32[24,2]{0,1:T(2,128)}, u32[]{:S(2)}) copy-start(s32[24,2]{0,1:T(2,128)} %param.8) | copy-start | bytes 580
  0.6 11.0 %copy-start = (bf16[24,4096]{1,0:T(8,128)(2,1)S(1)}, bf16[24,4096]{1,0:T(8,128)(2,1)}, u32[]{:S(2)}) copy-start(bf16[24,4096]{1,0:T(8,128)(2,1)} %param.7) | copy-start | bytes 589828
  0.7 11.0 %collective-permute-start = (s32[24,2]{0,1:T(2,128)}, s32[24,2]{0,1:T(2,128)S(1)}, u32[]{:S(2)}, u32[]{:S(2)}) collective-permute-start(s32[24,2]{0,1:T(2,128)} %param.8), channel_id=1, source_target_pairs={{0,1},{1,0},{2,3},{3,2},{4,5},{5,4},{6,7},{7,6},{8,9},{9,8},{10,11... | collective-permute-start | bytes 584 | tf_op jit(solution)/shard_map/ppermute | solution.py:369
  1.2 10.9 %collective-permute-start.8 = (bf16[24,4096]{1,0:T(8,128)(2,1)}, bf16[24,4096]{1,0:T(8,128)(2,1)S(1)}, u32[]{:S(2)}, u32[]{:S(2)}) collective-permute-start(bf16[24,4096]{1,0:T(8,128)(2,1)} %param.7), channel_id=1, source_target_pairs={{0,1},{1,0},{2,3},{3,2},{4,5},{5,4},{6,7},{7,6},{8,9},{9,8},{10,11... | collective-permute-start | bytes 589832 | tf_op jit(solution)/shard_map/ppermute | solution.py:369
  11.1 4.6 %collective-permute-start.1 = (bf16[512,2048]{1,0:T(8,128)(2,1)}, bf16[512,2048]{1,0:T(8,128)(2,1)}, u32[]{:S(2)}, u32[]{:S(2)}) collective-permute-start(bf16[512,2048]{1,0:T(8,128)(2,1)} %get-tuple-element.14), channel_id=1, source_target_pairs={{0,1},{1,0},{2,3},{3,2},{4,5},{5,4},{6,7},{7,6},{8,9},{9,8},{10,11... | collective-permute-start | bytes 6291464 | tf_op jit(solution)/shard_map/ppermute | solution.py:369
  23.8 15.7 %collective-permute-start.2 = (bf16[256,2048]{1,0:T(8,128)(2,1)S(1)}, bf16[256,2048]{1,0:T(8,128)(2,1)S(1)}, u32[]{:S(2)}, u32[]{:S(2)}) collective-permute-start(bf16[256,2048]{1,0:T(8,128)(2,1)S(1)} %get-tuple-element.16), channel_id=1, source_target_pairs={{0,4},{1,3},{2,6},{3,1},{4,0},{5,7},{6,2},{7,5},{8,12},{9,11},{10,... | collective-permute-start | bytes 3145736 | tf_op jit(solution)/shard_map/ppermute | solution.py:375
  26.8 7.5 %collective-permute-start.9 = (bf16[32,2048]{1,0:T(8,128)(2,1)S(1)}, bf16[32,2048]{1,0:T(8,128)(2,1)S(1)}, u32[]{:S(2)}, u32[]{:S(2)}) collective-permute-start(bf16[32,2048]{1,0:T(8,128)(2,1)S(1)} %get-tuple-element.23), channel_id=1, source_target_pairs={{0,24},{8,0},{16,8},{24,16},{1,25},{9,1},{17,9},{25,17},{2,26},{10... | collective-permute-start | bytes 393224 | tf_op jit(solution)/shard_map/ppermute | solution.py:378
  30.4 8.2 %collective-permute-start.11 = (bf16[32,2048]{1,0:T(8,128)(2,1)S(1)}, bf16[32,2048]{1,0:T(8,128)(2,1)S(1)}, u32[]{:S(2)}, u32[]{:S(2)}) collective-permute-start(bf16[32,2048]{1,0:T(8,128)(2,1)S(1)} %get-tuple-element.24), channel_id=1, source_target_pairs={{0,8},{8,16},{16,24},{24,0},{1,9},{9,17},{17,25},{25,1},{2,10},{10... | collective-permute-start | bytes 393224 | tf_op jit(solution)/shard_map/ppermute | solution.py:378
  30.4 11.5 %collective-permute-start.10 = (bf16[32,2048]{1,0:T(8,128)(2,1)S(1)}, bf16[32,2048]{1,0:T(8,128)(2,1)S(1)}, u32[]{:S(2)}, u32[]{:S(2)}) collective-permute-start(bf16[32,2048]{1,0:T(8,128)(2,1)S(1)} %get-tuple-element.25), channel_id=1, source_target_pairs={{0,16},{8,24},{16,0},{24,8},{1,17},{9,25},{17,1},{25,9},{2,18},{10... | collective-permute-start | bytes 393224 | tf_op jit(solution)/shard_map/ppermute | solution.py:378
  39.7 14.4 %collective-permute-start.3 = (bf16[128,2048]{1,0:T(8,128)(2,1)S(1)}, bf16[128,2048]{1,0:T(8,128)(2,1)S(1)}, u32[]{:S(2)}, u32[]{:S(2)}) collective-permute-start(bf16[128,2048]{1,0:T(8,128)(2,1)S(1)} %add_convert_fusion.1), channel_id=1, source_target_pairs={{0,2},{1,5},{2,0},{3,7},{4,6},{5,1},{6,4},{7,3},{8,10},{9,13},{10,... | collective-permute-start | bytes 1572872 | tf_op jit(solution)/shard_map/ppermute | solution.py:375
  41.9 9.2 %collective-permute-start.20 = (bf16[128,1024]{1,0:T(8,128)(2,1)S(1)}, bf16[128,1024]{1,0:T(8,128)(2,1)S(1)}, u32[]{:S(2)}, u32[]{:S(2)}) collective-permute-start(bf16[128,1024]{1,0:T(8,128)(2,1)S(1)} %pad_maximum_fusion.1.refs_0_), channel_id=1, source_target_pairs={{0,4},{1,3},{2,6},{3,1},{4,0},{5,7},{6,2},{7,5},{8,12},{9,11},{10,... | collective-permute-start | bytes 786440 | tf_op jit(solution)/shard_map/ppermute | solution.py:375
  43.5 13.3 %collective-permute-start.13 = (bf16[128,1024]{1,0:T(8,128)(2,1)S(1)}, bf16[128,1024]{1,0:T(8,128)(2,1)S(1)}, u32[]{:S(2)}, u32[]{:S(2)}) collective-permute-start(bf16[128,1024]{1,0:T(8,128)(2,1)S(1)} %pad_maximum_fusion.refs_0_), channel_id=1, source_target_pairs={{0,4},{1,3},{2,6},{3,1},{4,0},{5,7},{6,2},{7,5},{8,12},{9,11},{10,... | collective-permute-start | bytes 786440 | tf_op jit(solution)/shard_map/ppermute | solution.py:375
  44.1 13.2 %collective-permute-start.12 = (bf16[128,1024]{1,0:T(8,128)(2,1)S(1)}, bf16[128,1024]{1,0:T(8,128)(2,1)S(1)}, u32[]{:S(2)}, u32[]{:S(2)}) collective-permute-start(bf16[128,1024]{1,0:T(8,128)(2,1)S(1)} %pad_maximum_fusion.refs_0_), channel_id=1, source_target_pairs={{0,2},{1,5},{2,0},{3,7},{4,6},{5,1},{6,4},{7,3},{8,10},{9,13},{10,... | collective-permute-start | bytes 786440 | tf_op jit(solution)/shard_map/ppermute | solution.py:375
  44.9 18.1 %collective-permute-start.22 = (bf16[128,1024]{1,0:T(8,128)(2,1)S(1)}, bf16[128,1024]{1,0:T(8,128)(2,1)S(1)}, u32[]{:S(2)}, u32[]{:S(2)}) collective-permute-start(bf16[128,1024]{1,0:T(8,128)(2,1)S(1)} %pad_maximum_fusion.1.refs_0_), channel_id=1, source_target_pairs={{0,1},{1,0},{2,3},{3,2},{4,5},{5,4},{6,7},{7,6},{8,9},{9,8},{10,11... | collective-permute-start | bytes 786440 | tf_op jit(solution)/shard_map/ppermute | solution.py:369
  51.2 9.0 %collective-permute-start.19 = (bf16[128,1024]{1,0:T(8,128)(2,1)S(1)}, bf16[128,1024]{1,0:T(8,128)(2,1)S(1)}, u32[]{:S(2)}, u32[]{:S(2)}) collective-permute-start(bf16[128,1024]{1,0:T(8,128)(2,1)S(1)} %pad_maximum_fusion.1.refs_0_), channel_id=1, source_target_pairs={{0,2},{1,5},{2,0},{3,7},{4,6},{5,1},{6,4},{7,3},{8,10},{9,13},{10,... | collective-permute-start | bytes 786440 | tf_op jit(solution)/shard_map/ppermute | solution.py:375
  54.1 8.9 %collective-permute-start.21 = (bf16[128,1024]{1,0:T(8,128)(2,1)S(1)}, bf16[128,1024]{1,0:T(8,128)(2,1)S(1)}, u32[]{:S(2)}, u32[]{:S(2)}) collective-permute-start(bf16[128,1024]{1,0:T(8,128)(2,1)S(1)} %collective-permute-done.20.refs_2_), channel_id=1, source_target_pairs={{0,2},{1,5},{2,0},{3,7},{4,6},{5,1},{6,4},{7,3},{8,10},{9,13},{10,... | collective-permute-start | bytes 786440 | tf_op jit(solution)/shard_map/ppermute | solution.py:375
  56.8 11.7 %collective-permute-start.23 = (bf16[128,1024]{1,0:T(8,128)(2,1)S(1)}, bf16[128,1024]{1,0:T(8,128)(2,1)S(1)}, u32[]{:S(2)}, u32[]{:S(2)}) collective-permute-start(bf16[128,1024]{1,0:T(8,128)(2,1)S(1)} %collective-permute-done.20.refs_2_), channel_id=1, source_target_pairs={{0,1},{1,0},{2,3},{3,2},{4,5},{5,4},{6,7},{7,6},{8,9},{9,8},{10,11... | collective-permute-start | bytes 786440 | tf_op jit(solution)/shard_map/ppermute | solution.py:369
  57.3 9.7 %collective-permute-start.14 = (bf16[128,1024]{1,0:T(8,128)(2,1)S(1)}, bf16[128,1024]{1,0:T(8,128)(2,1)S(1)}, u32[]{:S(2)}, u32[]{:S(2)}) collective-permute-start(bf16[128,1024]{1,0:T(8,128)(2,1)S(1)} %collective-permute-done.13.refs_2_), channel_id=1, source_target_pairs={{0,2},{1,5},{2,0},{3,7},{4,6},{5,1},{6,4},{7,3},{8,10},{9,13},{10,... | collective-permute-start | bytes 786440 | tf_op jit(solution)/shard_map/ppermute | solution.py:375
  60.1 8.4 %collective-permute-start.24 = (bf16[128,1024]{1,0:T(8,128)(2,1)S(1)}, bf16[128,1024]{1,0:T(8,128)(2,1)S(1)}, u32[]{:S(2)}, u32[]{:S(2)}) collective-permute-start(bf16[128,1024]{1,0:T(8,128)(2,1)S(1)} %collective-permute-done.19.refs_1_), channel_id=1, source_target_pairs={{0,1},{1,0},{2,3},{3,2},{4,5},{5,4},{6,7},{7,6},{8,9},{9,8},{10,11... | collective-permute-start | bytes 786440 | tf_op jit(solution)/shard_map/ppermute | solution.py:369
  62.9 6.1 %collective-permute-start.25 = (bf16[128,1024]{1,0:T(8,128)(2,1)S(1)}, bf16[128,1024]{1,0:T(8,128)(2,1)S(1)}, u32[]{:S(2)}, u32[]{:S(2)}) collective-permute-start(bf16[128,1024]{1,0:T(8,128)(2,1)S(1)} %collective-permute-done.21.refs_3_), channel_id=1, source_target_pairs={{0,1},{1,0},{2,3},{3,2},{4,5},{5,4},{6,7},{7,6},{8,9},{9,8},{10,11... | collective-permute-start | bytes 786440 | tf_op jit(solution)/shard_map/ppermute | solution.py:369
  63.0 7.9 %collective-permute-start.6 = (bf16[32,2048]{1,0:T(8,128)(2,1)S(1)}, bf16[32,2048]{1,0:T(8,128)(2,1)S(1)}, u32[]{:S(2)}, u32[]{:S(2)}) collective-permute-start(bf16[32,2048]{1,0:T(8,128)(2,1)S(1)} %get-tuple-element.27), channel_id=1, source_target_pairs={{0,24},{8,0},{16,8},{24,16},{1,25},{9,1},{17,9},{25,17},{2,26},{10... | collective-permute-start | bytes 393224 | tf_op jit(solution)/shard_map/ppermute | solution.py:378
  67.0 9.3 %collective-permute-start.5 = (bf16[32,2048]{1,0:T(8,128)(2,1)S(1)}, bf16[32,2048]{1,0:T(8,128)(2,1)S(1)}, u32[]{:S(2)}, u32[]{:S(2)}) collective-permute-start(bf16[32,2048]{1,0:T(8,128)(2,1)S(1)} %get-tuple-element.28), channel_id=1, source_target_pairs={{0,16},{8,24},{16,0},{24,8},{1,17},{9,25},{17,1},{25,9},{2,18},{10... | collective-permute-start | bytes 393224 | tf_op jit(solution)/shard_map/ppermute | solution.py:378
  68.5 16.5 %collective-permute-start.15 = (bf16[128,1024]{1,0:T(8,128)(2,1)S(1)}, bf16[128,1024]{1,0:T(8,128)(2,1)S(1)}, u32[]{:S(2)}, u32[]{:S(2)}) collective-permute-start(bf16[128,1024]{1,0:T(8,128)(2,1)S(1)} %pad_maximum_fusion.refs_0_), channel_id=1, source_target_pairs={{0,1},{1,0},{2,3},{3,2},{4,5},{5,4},{6,7},{7,6},{8,9},{9,8},{10,11... | collective-permute-start | bytes 786440 | tf_op jit(solution)/shard_map/ppermute | solution.py:369
  68.5 16.5 %collective-permute-start.16 = (bf16[128,1024]{1,0:T(8,128)(2,1)S(1)}, bf16[128,1024]{1,0:T(8,128)(2,1)S(1)}, u32[]{:S(2)}, u32[]{:S(2)}) collective-permute-start(bf16[128,1024]{1,0:T(8,128)(2,1)S(1)} %collective-permute-done.13.refs_2_), channel_id=1, source_target_pairs={{0,1},{1,0},{2,3},{3,2},{4,5},{5,4},{6,7},{7,6},{8,9},{9,8},{10,11... | collective-permute-start | bytes 786440 | tf_op jit(solution)/shard_map/ppermute | solution.py:369
  69.0 16.0 %collective-permute-start.17 = (bf16[128,1024]{1,0:T(8,128)(2,1)S(1)}, bf16[128,1024]{1,0:T(8,128)(2,1)S(1)}, u32[]{:S(2)}, u32[]{:S(2)}) collective-permute-start(bf16[128,1024]{1,0:T(8,128)(2,1)S(1)} %collective-permute-done.12.refs_1_), channel_id=1, source_target_pairs={{0,1},{1,0},{2,3},{3,2},{4,5},{5,4},{6,7},{7,6},{8,9},{9,8},{10,11... | collective-permute-start | bytes 786440 | tf_op jit(solution)/shard_map/ppermute | solution.py:369
  70.9 14.1 %collective-permute-start.18 = (bf16[128,1024]{1,0:T(8,128)(2,1)S(1)}, bf16[128,1024]{1,0:T(8,128)(2,1)S(1)}, u32[]{:S(2)}, u32[]{:S(2)}) collective-permute-start(bf16[128,1024]{1,0:T(8,128)(2,1)S(1)} %collective-permute-done.14.refs_3_), channel_id=1, source_target_pairs={{0,1},{1,0},{2,3},{3,2},{4,5},{5,4},{6,7},{7,6},{8,9},{9,8},{10,11... | collective-permute-start | bytes 786440 | tf_op jit(solution)/shard_map/ppermute | solution.py:369
  76.3 8.4 %collective-permute-start.4 = (bf16[32,2048]{1,0:T(8,128)(2,1)S(1)}, bf16[32,2048]{1,0:T(8,128)(2,1)S(1)}, u32[]{:S(2)}, u32[]{:S(2)}) collective-permute-start(bf16[32,2048]{1,0:T(8,128)(2,1)S(1)} %get-tuple-element.29), channel_id=1, source_target_pairs={{0,8},{8,16},{16,24},{24,0},{1,9},{9,17},{17,25},{25,1},{2,10},{10... | collective-permute-start | bytes 393224 | tf_op jit(solution)/shard_map/ppermute | solution.py:378
  84.9 7.5 %collective-permute-start.7 = (bf16[24,2048]{1,0:T(8,128)(2,1)S(1)}, bf16[24,2048]{1,0:T(8,128)(2,1)S(1)}, u32[]{:S(2)}, u32[]{:S(2)}) collective-permute-start(bf16[24,2048]{1,0:T(8,128)(2,1)S(1)} %slice.110), channel_id=1, source_target_pairs={{0,1},{1,0},{2,3},{3,2},{4,5},{5,4},{6,7},{7,6},{8,9},{9,8},{10,11... | collective-permute-start | bytes 294920 | tf_op jit(solution)/shard_map/ppermute | solution.py:369
